TPU v7x, 768 devices: a whole 4x8x12 slice. The times are simulated.
768 devices in a mesh: dp: 12 (over z), mp: 64 (over y, x, core).
Axes of the slice: x: 4, y: 8, z: 12, core: 2. Of those that a mesh axis runs over, the one named last changes fastest.
Arguments:
- grad_partial: bfloat16 [12, 32, 576, 576], P('dp', None, 'mp'), may hold values from -1.796875 to 1.796875
- owner: int32 [32], replicated, may hold values from 0 to 63, as said below
- offset: int32 [32], replicated, may hold values from 0 to 31, each once
- left_factor: float32 [64, 576, 576], P('mp', None, 'dp'), may hold values from -3 to 3
- right_factor: float32 [64, 576, 576], P('mp', None, 'dp'), may hold values from -3 to 3
- left_basis: bfloat16 [64, 576, 576], P('mp'), may hold values from -0.25 to 0.25
- right_basis: bfloat16 [64, 576, 576], P('mp'), may hold values from -0.25 to 0.25
- momentum: bfloat16 [64, 576, 576], P('mp'), may hold values from -6 to 6
- second_moment: float32 [64, 576, 576], P('mp'), may hold values from 0.2 to 2
Outputs:
- update: bfloat16 [32, 576, 576], P(None, 'mp', 'dp')
- new_left: float32 [64, 576, 576], P('mp', None, 'dp')
- new_right: float32 [64, 576, 576], P('mp', None, 'dp')
- new_momentum: bfloat16 [64, 576, 576], P('mp')
- new_second: float32 [64, 576, 576], P('mp')
Inputs may be any that keep to these rules, and one draw needn't show every extreme that they name: No two blocks have the same owner. `offset`: every position belongs to exactly one block.
All inputs are finite; a program needn't handle non-finite values.
Results may differ from a plain program's by a relative error of at most 0.015.
Values may be sent and summed in bfloat16 or wider, within the bound.
A program may use at most 32 MiB of HBM per device.

v0:
```python
import jax
import jax.numpy as jnp
from jax import lax
from jax.sharding import PartitionSpec as P


def contract_first(matrix_a, matrix_b):
    return lax.dot_general(
        matrix_a, matrix_b, (((0,), (0,)), ((), ())), preferred_element_type=jnp.float32
    )


def contract_last(matrix_a, matrix_b):
    return lax.dot_general(
        matrix_a, matrix_b, (((1,), (1,)), ((), ())), preferred_element_type=jnp.float32
    )


def per_device(
    grad_partial,
    owner,
    offset,
    left_factor,
    right_factor,
    left_basis,
    right_basis,
    momentum,
    second_moment,
):
    pieces = grad_partial[0]
    blocks, row_count, columns = pieces.shape
    groups = lax.axis_size("mp")
    replicas = lax.axis_size("dp")
    col_share = columns // replicas
    column = lax.axis_index("dp") * col_share
    my_group = lax.axis_index("mp")
    targets = lax.broadcasted_iota(jnp.int32, (groups, blocks), 0)
    positions = lax.broadcasted_iota(jnp.int32, (blocks, blocks), 0)
    routing = (owner[None, :] == targets).astype(jnp.float32)
    where_at = (offset[None, :] == positions).astype(jnp.float32)
    select = contract_last(routing, where_at).astype(jnp.bfloat16)
    occupied = jnp.any(owner == my_group)
    swapped = lax.all_to_all(grad_partial, "dp", split_axis=3, concat_axis=0, tiled=True)
    summed = jnp.sum(swapped.astype(jnp.float32), axis=0).astype(jnp.bfloat16)
    outgoing = jnp.dot(
        select, summed.reshape(blocks, row_count * col_share), preferred_element_type=jnp.float32
    )
    outgoing = outgoing.astype(jnp.bfloat16).reshape(groups, row_count, col_share)
    landed = lax.all_to_all(outgoing, "mp", split_axis=0, concat_axis=0, tiled=True)
    arrived = lax.all_gather(landed, "dp", axis=2, tiled=True)
    gradient = arrived.reshape(groups * row_count, columns)

    def refresh(operands):
        grad_in, left_fac, right_fac, lbasis, rbasis, moment, second = operands
        grad_rows = lax.dynamic_slice_in_dim(grad_in, column, col_share, 0)
        grad_cols = lax.dynamic_slice_in_dim(grad_in, column, col_share, 1)
        new_left = 0.95 * left_fac + 0.05 * contract_last(grad_in, grad_rows)
        new_right = 0.95 * right_fac + 0.05 * contract_first(grad_in, grad_cols)
        new_moment = (0.9 * moment.astype(jnp.float32) + 0.1 * grad_in.astype(jnp.float32)).astype(
            jnp.bfloat16
        )
        turned = contract_first(lbasis, grad_in).astype(jnp.bfloat16)
        rotated = jnp.dot(turned, rbasis, preferred_element_type=jnp.float32)
        turned_mom = contract_first(lbasis, new_moment).astype(jnp.bfloat16)
        rotated_mom = jnp.dot(turned_mom, rbasis, preferred_element_type=jnp.float32)
        new_second = 0.95 * second + 0.05 * rotated * rotated
        scaled = (rotated_mom / (jnp.sqrt(new_second) + 1e-08)).astype(jnp.bfloat16)
        unrotated = jnp.dot(lbasis, scaled, preferred_element_type=jnp.float32).astype(jnp.bfloat16)
        back_rows = lax.dynamic_slice_in_dim(rbasis, column, col_share, 0)
        return (new_left, new_right, new_moment, new_second, contract_last(unrotated, back_rows))

    def keep_old(operands):
        grad_in, left_fac, right_fac, lbasis, rbasis, moment, second = operands
        return (left_fac, right_fac, moment, second, jnp.zeros((columns, col_share), jnp.float32))

    operands = (
        gradient,
        left_factor[0],
        right_factor[0],
        left_basis[0],
        right_basis[0],
        momentum[0],
        second_moment[0],
    )
    new_left, new_right, new_moment, new_second, turned_cols = lax.cond(
        occupied, refresh, keep_old, operands
    )
    outgoing_back = turned_cols.astype(jnp.bfloat16).reshape(groups, row_count, col_share)
    returned = lax.all_to_all(outgoing_back, "mp", split_axis=0, concat_axis=0, tiled=True)
    update = contract_first(select, returned.reshape(groups, row_count * col_share)).astype(
        jnp.bfloat16
    )
    update = update.reshape(blocks, row_count, col_share)
    return (update, new_left[None], new_right[None], new_moment[None], new_second[None])


def solution(mesh):
    placed = (
        P("dp", None, "mp", None),
        P(),
        P(),
        P("mp", None, "dp"),
        P("mp", None, "dp"),
        P("mp", None, None),
        P("mp", None, None),
        P("mp", None, None),
        P("mp", None, None),
    )
    return jax.shard_map(
        per_device,
        mesh=mesh,
        in_specs=placed,
        out_specs=(
            P(None, "mp", "dp"),
            P("mp", None, "dp"),
            P("mp", None, "dp"),
            P("mp", None, None),
            P("mp", None, None),
        ),
        check_vma=False,
    )
```

profile of v0, /device:TPU:1, one launch (start us, length us, event | category | flops | bytes accessed | tf_op | source)
XLA Modules:
  0.0 132.2 jit_solution(3632982349068195995)
XLA Ops:
  0.6 2.0 %copy.59 = bf16[1,576,576]{2,1,0:T(8,128)(2,1)} copy(bf16[1,576,576]{2,1,0:T(8,128)(2,1)} %param.18) | data formatting | bytes 1327104
  2.7 0.0 copy-start.9
  2.7 1.0 copy-done.9
  3.7 2.0 %copy.30 = bf16[1,32,9,576]{1,2,0,3:T(8,128)(2,1)S(1)} copy(bf16[1,32,9,576]{3,1,2,0:T(8,128)(2,1)S(1)} %copy-done.9) | data formatting | bytes 663552 | tf_op args[0]
  5.7 0.0 copy-start.11
  5.7 0.0 copy-start.12
  5.7 2.1 %reshape.40 = bf16[12,2,6912]{2,1,0:T(2,128)(2,1)} reshape(bf16[576,1,9,32]{3,2,1,0:T(8,128)(2,1)S(1)} %bitcast.49) | data formatting | bytes 663552
  7.8 15.7 %all-to-all-start = ((bf16[12,2,6912]{2,1,0:T(2,128)(2,1)}), bf16[12,2,6912]{2,1,0:T(2,128)(2,1)S(1)}, u32[]{:S(2)}, u32[]{:S(2)}) async-start(bf16[12,2,6912]{2,1,0:T(2,128)(2,1)} %reshape.40), calls=%async_computation | async-start | bytes 663552 | tf_op jit(solution)/shard_map/all_to_all | solution.py:43
  23.5 0.0 copy-done.11
  23.5 0.0 copy-done.12
  23.6 0.1 convolution_convert_fusion.5
  23.7 16.7 %all-to-all-done = bf16[12,2,6912]{2,1,0:T(2,128)(2,1)S(1)} async-done(((bf16[12,2,6912]{2,1,0:T(2,128)(2,1)}), bf16[12,2,6912]{2,1,0:T(2,128)(2,1)S(1)}, u32[]{:S(2)}, u32[]{:S(2)}) %all-to-all-start) | async-done | bytes 331808 | tf_op jit(solution)/shard_map/all_to_all | solution.py:43
  40.4 1.3 %reshape.41 = bf16[576,1,9,32]{3,2,1,0:T(8,128)(2,1)S(1)} reshape(bf16[12,2,6912]{2,1,0:T(2,128)(2,1)S(1)} %all-to-all-done) | data formatting | bytes 663552
  41.7 0.6 reduce_sum.12
  42.3 0.3 copy.32
  42.6 0.1 reshape.35
  42.7 0.2 convolution_convert_fusion.3
  42.9 0.1 copy.33
  43.0 0.0 copy-start.4
  43.1 0.0 copy-start.6
  43.1 0.0 copy-start.8
  43.1 0.3 copy.34
  43.3 0.8 reshape.42
  44.2 12.3 %all-to-all-start.1 = ((bf16[64,2,216]{2,1,0:T(2,128)(2,1)}), bf16[64,2,216]{2,1,0:T(2,128)(2,1)S(1)}, u32[]{:S(2)}, u32[]{:S(2)}) async-start(bf16[64,2,216]{2,1,0:T(2,128)(2,1)} %reshape.42), calls=%async_computation.1 | async-start | bytes 131072 | tf_op jit(solution)/shard_map/all_to_all | solution.py:49
  56.5 0.6 compare_reduce_fusion
  57.8 8.8 %all-to-all-done.1 = bf16[64,2,216]{2,1,0:T(2,128)(2,1)S(1)} async-done(((bf16[64,2,216]{2,1,0:T(2,128)(2,1)}), bf16[64,2,216]{2,1,0:T(2,128)(2,1)S(1)}, u32[]{:S(2)}, u32[]{:S(2)}) %all-to-all-start.1) | async-done | bytes 55328 | tf_op jit(solution)/shard_map/all_to_all | solution.py:49
  66.6 0.3 reshape.43
  66.8 0.2 copy.35
  67.1 25.4 %all_gather.3 = bf16[64,9,576]{0,2,1:T(8,128)(2,1)S(1)} all-gather(bf16[64,9,48]{0,2,1:T(8,128)(2,1)S(1)} %copy.35), channel_id=1, replica_groups=mesh['dp'=12,'mp'=64] {'dp'}, dimensions={2}, use_global_device_ids=true | all-gather | bytes 718848 | tf_op jit(solution)/shard_map/all_gather | solution.py:50
  92.4 0.0 copy-done.4
  92.4 0.0 copy-done.6
  92.4 0.0 copy-done.8
  92.5 0.0 copy-start.3
  92.5 0.0 copy-start.5
  92.5 0.0 copy-start.7
  92.5 0.1 copy.37
  92.7 0.1 reshape.37
  92.7 0.2 reshape.44
  92.9 37.8 %all_to_all.22 = bf16[64,2,216]{2,1,0:T(2,128)(2,1)S(1)} all-to-all(bf16[64,2,216]{2,1,0:T(2,128)(2,1)S(1)} %reshape.44), channel_id=1, replica_groups=mesh['dp'=12,'mp'=64] {'mp'}, dimensions={0} | all-to-all | bytes 110592 | tf_op jit(solution)/shard_map/all_to_all | solution.py:89
  130.8 0.3 reshape.45
  131.0 0.2 copy.38
  131.2 0.2 convolution_convert_fusion.4
  131.4 0.1 reshape.39
  131.6 0.7 copy.39
  132.2 0.0 copy-done.3
  132.2 0.0 copy-done.5
  132.2 0.0 copy-done.7
  (2 shorter events, 0.0 us)
Async XLA Ops:
  2.7 1.0 copy-start.9
  5.7 17.8 %copy-start.11 = (s32[32]{0:T(128)S(1)}, s32[32]{0:T(128)}, u32[]{:S(2)}) copy-start(s32[32]{0:T(128)} %param.13) | copy-start | bytes 388
  5.7 17.8 %copy-start.12 = (s32[32]{0:T(128)S(1)}, s32[32]{0:T(128)}, u32[]{:S(2)}) copy-start(s32[32]{0:T(128)} %param.12) | copy-start | bytes 388
  7.8 32.6 %all-to-all-start = ((bf16[12,2,6912]{2,1,0:T(2,128)(2,1)}), bf16[12,2,6912]{2,1,0:T(2,128)(2,1)S(1)}, u32[]{:S(2)}, u32[]{:S(2)}) async-start(bf16[12,2,6912]{2,1,0:T(2,128)(2,1)} %reshape.40), calls=%async_computation | async-start | bytes 663552 | tf_op jit(solution)/shard_map/all_to_all | solution.py:43
  43.0 49.4 %copy-start.4 = (f32[1,576,576]{2,1,0:T(8,128)S(1)}, f32[1,576,576]{2,1,0:T(8,128)}, u32[]{:S(2)}) copy-start(f32[1,576,576]{2,1,0:T(8,128)} %param.19) | copy-start | bytes 3981316
  43.1 49.4 %copy-start.6 = (f32[1,576,48]{1,2,0:T(8,128)S(1)}, f32[1,576,48]{1,2,0:T(8,128)}, u32[]{:S(2)}) copy-start(f32[1,576,48]{1,2,0:T(8,128)} %param.14) | copy-start | bytes 331780
  43.1 49.4 %copy-start.8 = (f32[1,576,48]{1,2,0:T(8,128)S(1)}, f32[1,576,48]{1,2,0:T(8,128)}, u32[]{:S(2)}) copy-start(f32[1,576,48]{1,2,0:T(8,128)} %param.15) | copy-start | bytes 331780
  44.2 22.4 %all-to-all-start.1 = ((bf16[64,2,216]{2,1,0:T(2,128)(2,1)}), bf16[64,2,216]{2,1,0:T(2,128)(2,1)S(1)}, u32[]{:S(2)}, u32[]{:S(2)}) async-start(bf16[64,2,216]{2,1,0:T(2,128)(2,1)} %reshape.42), calls=%async_computation.1 | async-start | bytes 131072 | tf_op jit(solution)/shard_map/all_to_all | solution.py:49
  92.5 39.8 %copy-start.3 = (f32[576,576]{1,0:T(8,128)}, f32[576,576]{1,0:T(8,128)S(1)}, u32[]{:S(2)}) copy-start(f32[576,576]{1,0:T(8,128)S(1)} %get-tuple-element.71) | copy-start | bytes 3981316
  92.5 39.7 %copy-start.5 = (f32[576,48]{0,1:T(8,128)}, f32[576,48]{0,1:T(8,128)S(1)}, u32[]{:S(2)}) copy-start(f32[576,48]{0,1:T(8,128)S(1)} %get-tuple-element.68) | copy-start | bytes 331780
  92.5 39.7 %copy-start.7 = (f32[576,48]{0,1:T(8,128)}, f32[576,48]{0,1:T(8,128)S(1)}, u32[]{:S(2)}) copy-start(f32[576,48]{0,1:T(8,128)S(1)} %get-tuple-element.69) | copy-start | bytes 331780
where the time goes:
time: 133 us; the launch traced here: 132 us
  blocking collectives  63.2 us (48%)
  starting transfers between devices  28 us (21%)
  waiting for transfers between devices  25.5 us (19%)
  local copies, waits for them, and re-layouts  12.3 us (9%)
  between operations  1.49 us (1%)
    all_to_all x1, blocking collectives, per_device(): lax.all_to_all(outgoing_back, 'mp', split_axis=0, concat_axis=0, tiled=True)  37.8 us
    all_gather x1, blocking collectives, per_device(): arrived = lax.all_gather(landed, 'dp', axis=2, tiled=True)  25.4 us
    all_to_all x1, waiting for transfers between devices, per_device(): lax.all_to_all(grad_partial, 'dp', split_axis=3, concat_axis=0, tiled=True)  16.7 us
    all_to_all x1, starting transfers between devices, per_device(): lax.all_to_all(grad_partial, 'dp', split_axis=3, concat_axis=0, tiled=True)  15.7 us
    all_to_all x1, starting transfers between devices, per_device(): lax.all_to_all(outgoing, 'mp', split_axis=0, concat_axis=0, tiled=True)  12.3 us
    unnamed x27, local copies, waits for them, and re-layouts  10.8 us
    all_to_all x1, waiting for transfers between devices, per_device(): lax.all_to_all(outgoing, 'mp', split_axis=0, concat_axis=0, tiled=True)  8.8 us
  transfers between devices with their start and end apart: 2, of which 2 were waited for; matrix products, arithmetic and copies ran while one was open for 1% of the time, Pallas kernels for 0%

commit v1 on v0

v1 whole, which is shorter than its diff:
```python
import functools

import jax
import jax.numpy as jnp
from jax import lax
from jax.experimental import pallas as pl
from jax.experimental.pallas import tpu as pltpu
from jax.sharding import PartitionSpec as P

MESH = pl.DeviceIdType.MESH
F32 = jnp.float32
BF16 = jnp.bfloat16

BS = 576
NB = 32
ND = 12
NM = 64
RPD = BS // NM
CPD = BS // ND
LANES = 128
TILES = 5
UNITS = RPD * TILES
PER = 4
HALF = ND // 2

STARTS = [(UNITS * s) // ND for s in range(ND + 1)]
SLOT_OF = {}
for _s in range(ND):
    for _u in range(STARTS[_s], STARTS[_s + 1]):
        SLOT_OF[_u] = _s * PER + _u - STARTS[_s]


def mm(a, b):
    return lax.dot_general(a, b, (((1,), (0,)), ((), ())), preferred_element_type=F32)


def mm_nt(a, b):
    return lax.dot_general(a, b, (((1,), (1,)), ((), ())), preferred_element_type=F32)


def grid2(rows, cols):
    return (
        lax.broadcasted_iota(jnp.int32, (rows, cols), 0),
        lax.broadcasted_iota(jnp.int32, (rows, cols), 1),
    )


def one_hot(mask):
    return jnp.where(mask, 1.0, 0.0).astype(BF16)


def wrap(x, n):
    return lax.rem(x, n)


def kernel(
    gp_hbm, owner_ref, offset_ref, lf_hbm, rf_hbm, lb_hbm, rb_hbm, mom_hbm, sec_hbm,
    upd_hbm, nlf_hbm, nrf_hbm, nmom_hbm, nsec_hbm,
    gp, lf, rf, lb, rb, mom, sec,
    sbuf, land1, out2, land2, gu, out4, land4,
    gn, lbt, lbp, tm, nmom, scaled, nlf, nrf, upd,
    load_sem, store_sem, s1_send, s1_recv, s2_send, s2_recv, s3_send, s3_recv, s4_send, s4_recv,
):
    me_z = lax.axis_index("dp")
    me_m = lax.axis_index("mp")

    loads = [
        pltpu.make_async_copy(src, dst, load_sem.at[i])
        for i, (src, dst) in enumerate(
            ((gp_hbm, gp), (lb_hbm, lb), (rb_hbm, rb), (mom_hbm, mom), (sec_hbm, sec), (lf_hbm, lf), (rf_hbm, rf))
        )
    ]
    for copy in loads:
        copy.start()

    barrier = pltpu.get_barrier_semaphore()

    def greet_z(i, carry):
        pl.semaphore_signal(barrier, inc=1, device_id=(wrap(me_z + i, ND), me_m), device_id_type=MESH)
        return carry

    def greet_m(i, carry):
        pl.semaphore_signal(barrier, inc=1, device_id=(me_z, wrap(me_m + i, NM)), device_id_type=MESH)
        return carry

    lax.fori_loop(1, ND, greet_z, 0)
    lax.fori_loop(1, NM, greet_m, 0)

    loads[0].wait()
    for s in range(ND):
        for k in range(PER):
            u = STARTS[s] + k
            if u < STARTS[s + 1]:
                i, t = u // TILES, u % TILES
                if t < TILES - 1:
                    sbuf[s, k] = gp[i, :, t * LANES : (t + 1) * LANES]
                else:
                    sbuf[s, k] = jnp.zeros((NB, LANES), BF16)
                    sbuf[s, k, :, : BS - t * LANES] = gp[i, :, t * LANES : BS]
            else:
                sbuf[s, k] = jnp.zeros((NB, LANES), BF16)

    pl.semaphore_wait(barrier, ND - 1 + NM - 1)

    def copy1(i):
        to = wrap(me_z + i, ND)
        return pltpu.make_async_remote_copy(
            src_ref=sbuf.at[to], dst_ref=land1.at[me_z], send_sem=s1_send.at[i], recv_sem=s1_recv.at[me_z],
            device_id=(to, me_m), device_id_type=MESH,
        )

    def got1(i):
        frm = wrap(me_z + i, ND)
        return pltpu.make_async_remote_copy(
            src_ref=sbuf.at[frm], dst_ref=land1.at[frm], send_sem=s1_send.at[i], recv_sem=s1_recv.at[frm],
            device_id=(frm, me_m), device_id_type=MESH,
        )

    order = [x for d in range(HALF, 0, -1) for x in ((d, ND - d) if d != HALF else (d,))]
    for i in order:
        copy1(i).start()

    owner = owner_ref[...]
    offset = offset_ref[...]
    occupied = jnp.max(jnp.where(owner == me_m, 1.0, 0.0), axis=1, keepdims=True)
    keep_factor = jnp.where(occupied > 0.5, 0.95, 1.0)
    keep_mom = jnp.where(occupied > 0.5, 0.9, 1.0)
    add_factor = jnp.where(occupied > 0.5, 0.05, 0.0)
    add_mom = jnp.where(occupied > 0.5, 0.1, 0.0)

    row, col = grid2(NM * 8, NB)
    by_owner = one_hot(owner == row // 8)
    row, col = grid2(PER * NB, NB)
    by_offset = one_hot(offset == wrap(row, NB))
    row, col = grid2(NM * 8, PER * NB)
    route = jnp.where(wrap(row, 8) == col // NB, mm_nt(by_owner, by_offset), 0.0).astype(BF16)

    row, col = grid2(BS, BS)
    loads[1].wait()
    lbt[...] = mm_nt(one_hot(row == col), lb[...]).astype(BF16)
    slab = row // NM
    slab = jnp.where(slab < 5, 2 * slab, 2 * slab - 9)
    lbp[...] = mm(one_hot(col == wrap(row, NM) * RPD + slab), lb[...]).astype(BF16)
    for copy in loads[2:]:
        copy.wait()

    total = [sbuf[me_z, k].astype(F32) for k in range(PER)]
    for i in (1, 11, 2, 10, 3, 9, 4, 8, 5, 7, 6):
        got1(i).wait_recv()
        frm = wrap(me_z + i, ND)
        total = [total[k] + land1[frm, k].astype(F32) for k in range(PER)]
    summed = jnp.concatenate(total, axis=0).astype(BF16)

    out2[...] = mm(route, summed).reshape(NM, 8, LANES).astype(BF16)
    land2[me_m] = out2[me_m]

    def send2(i, carry):
        to = wrap(me_m + i, NM)
        pltpu.make_async_remote_copy(
            src_ref=out2.at[to], dst_ref=land2.at[me_m], send_sem=s2_send, recv_sem=s2_recv,
            device_id=(me_z, to), device_id_type=MESH,
        ).start()
        return carry

    lax.fori_loop(1, NM, send2, 0)
    done2 = pltpu.make_async_remote_copy(
        src_ref=out2.at[pl.ds(0, NM - 1)], dst_ref=land2.at[pl.ds(0, NM - 1)], send_sem=s2_send, recv_sem=s2_recv,
        device_id=(me_z, wrap(me_m + 1, NM)), device_id_type=MESH,
    )
    row, col = grid2(PER * NM, NM * 8)
    gather = one_hot(col == wrap(row, NM) * 8 + row // NM)
    done2.wait_recv()
    arrived = land2[...].astype(F32).reshape(NM * 8, LANES).astype(BF16)
    gu[pl.ds(me_z * PER, PER)] = mm(gather, arrived).astype(BF16).reshape(PER, NM, LANES)

    right = (wrap(me_z + 1, ND), me_m)
    left = (wrap(me_z + ND - 1, ND), me_m)

    def hop(way, dist, k):
        origin = wrap(me_z + (ND - dist + 1 if way == 0 else dist - 1), ND)
        slot = gu.at[origin * PER + k]
        return pltpu.make_async_remote_copy(
            src_ref=slot, dst_ref=slot, send_sem=s3_send.at[way, dist - 1, k], recv_sem=s3_recv.at[way, dist - 1, k],
            device_id=right if way == 0 else left, device_id_type=MESH,
        )

    def landed(way, dist, k):
        origin = wrap(me_z + (ND - dist if way == 0 else dist), ND)
        slot = gu.at[origin * PER + k]
        return pltpu.make_async_remote_copy(
            src_ref=slot, dst_ref=slot, send_sem=s3_send.at[way, dist - 1, k], recv_sem=s3_recv.at[way, dist - 1, k],
            device_id=right if way == 0 else left, device_id_type=MESH,
        )

    def goes(way, dist, k):
        return dist < HALF or (dist == HALF and (k < PER // 2) == (way == 0))

    for k in range(PER):
        for way in (0, 1):
            hop(way, 1, k).start()
    for dist in range(1, HALF + 1):
        for k in range(PER):
            for way in (0, 1):
                if goes(way, dist, k):
                    landed(way, dist, k).wait_recv()
                    if goes(way, dist + 1, k):
                        hop(way, dist + 1, k).start()

    row, col = grid2(BS, BS)
    to_rows = one_hot(row == wrap(col, NM) * RPD + col // NM)
    for t in range(TILES):
        tile = jnp.concatenate([gu[SLOT_OF[i * TILES + t]] for i in range(RPD)], axis=0)
        width = min(LANES, BS - t * LANES)
        gn[:, t * LANES : t * LANES + width] = mm(to_rows, tile).astype(BF16)[:, :width]

    nmom[...] = (keep_mom * mom[...].astype(F32) + add_mom * gn[...].astype(F32)).astype(BF16)
    tm[0] = mm(lbt[...], gn[...]).astype(BF16)
    tm[1] = mm(lbt[...], nmom[...]).astype(BF16)
    step = BS // 3
    for part in range(3):
        rows = slice(part * step, (part + 1) * step)
        rotated = mm(tm[0, rows], rb[...])
        rotated_mom = mm(tm[1, rows], rb[...])
        new_second = keep_factor * sec[rows, :] + add_factor * rotated * rotated
        sec[rows, :] = new_second
        scaled[rows, :] = (rotated_mom / (jnp.sqrt(new_second) + 1e-08)).astype(BF16)
    store_second = pltpu.make_async_copy(sec, nsec_hbm, store_sem.at[0])
    store_second.start()
    store_mom = pltpu.make_async_copy(nmom, nmom_hbm, store_sem.at[1])
    store_mom.start()

    unrotated = mm(lbp[...], scaled[...]).astype(BF16)
    back = rb[pl.ds(pl.multiple_of(me_z * CPD, 16), CPD), :]
    zeros = functools.partial(jnp.zeros, dtype=BF16)
    even = mm_nt(unrotated[: 5 * NM], jnp.concatenate([back, zeros((LANES - CPD, BS))], axis=0))
    odd = mm_nt(unrotated[5 * NM :], jnp.concatenate([zeros((CPD, BS)), back, zeros((LANES - 2 * CPD, BS))], axis=0))
    pairs = jnp.concatenate([even[: 4 * NM] + odd, even[4 * NM :]], axis=0).astype(BF16)
    row, col = grid2(NM * 8, 5 * NM)
    spread = one_hot(col == wrap(row, 8) * NM + row // 8)
    out4[...] = mm(spread, pairs).reshape(NM, 8, LANES).astype(BF16)
    land4[me_m] = out4[me_m]

    def send4(i, carry):
        to = wrap(me_m + i, NM)
        pltpu.make_async_remote_copy(
            src_ref=out4.at[to], dst_ref=land4.at[me_m], send_sem=s4_send, recv_sem=s4_recv,
            device_id=(me_z, to), device_id_type=MESH,
        ).start()
        return carry

    lax.fori_loop(1, NM, send4, 0)
    done4 = pltpu.make_async_remote_copy(
        src_ref=out4.at[pl.ds(0, NM - 1)], dst_ref=land4.at[pl.ds(0, NM - 1)], send_sem=s4_send, recv_sem=s4_recv,
        device_id=(me_z, wrap(me_m + 1, NM)), device_id_type=MESH,
    )

    my_rows = gn[pl.ds(pl.multiple_of(me_z * CPD, 16), CPD), :]
    nlf[...] = keep_factor * lf[...] + add_factor * mm_nt(my_rows, gn[...])
    row, col = grid2(CPD, BS)
    my_cols = mm_nt(one_hot(col == row + me_z * CPD), gn[...]).astype(BF16)
    nrf[...] = keep_factor * rf[...] + add_factor * mm(my_cols, gn[...])
    store_left = pltpu.make_async_copy(nlf, nlf_hbm, store_sem.at[2])
    store_left.start()
    store_right = pltpu.make_async_copy(nrf, nrf_hbm, store_sem.at[3])
    store_right.start()

    row, col = grid2(5 * NB, NB)
    at_offset = one_hot(offset == wrap(row, NB))
    row, col = grid2(5 * NB, NM * 8)
    place = jnp.where(row // NB == wrap(col, 8), mm_nt(at_offset, by_owner), 0.0).astype(BF16)

    done4.wait_recv()
    returned = land4[...].astype(F32).reshape(NM * 8, LANES).astype(BF16)
    placed = mm(place, returned).astype(BF16)
    for i in range(RPD):
        pair = placed[(i // 2) * NB : (i // 2 + 1) * NB, :]
        upd[i] = pair[:, (i % 2) * CPD : (i % 2 + 1) * CPD]
    store_update = pltpu.make_async_copy(upd, upd_hbm, store_sem.at[4])
    store_update.start()

    for i in range(1, ND):
        copy1(i).wait_send()
    done2.wait_send()
    for dist in range(1, HALF + 1):
        for k in range(PER):
            for way in (0, 1):
                if goes(way, dist, k):
                    hop(way, dist, k).wait_send()
    done4.wait_send()
    for copy in (store_second, store_mom, store_left, store_right, store_update):
        copy.wait()


def per_device(gp, owner, offset, lf, rf, lb, rb, mom, sec):
    anywhere = pl.BlockSpec(memory_space=pl.ANY)
    whole = pl.BlockSpec(memory_space=pltpu.VMEM)
    dma = pltpu.SemaphoreType.DMA
    outs = pl.pallas_call(
        kernel,
        out_shape=(
            jax.ShapeDtypeStruct((RPD, NB, CPD), BF16),
            jax.ShapeDtypeStruct((CPD, BS), F32),
            jax.ShapeDtypeStruct((CPD, BS), F32),
            jax.ShapeDtypeStruct((BS, BS), BF16),
            jax.ShapeDtypeStruct((BS, BS), F32),
        ),
        in_specs=[anywhere, whole, whole] + [anywhere] * 6,
        out_specs=[anywhere] * 5,
        scratch_shapes=[
            pltpu.VMEM((RPD, NB, BS), BF16),
            pltpu.VMEM((CPD, BS), F32),
            pltpu.VMEM((CPD, BS), F32),
            pltpu.VMEM((BS, BS), BF16),
            pltpu.VMEM((BS, BS), BF16),
            pltpu.VMEM((BS, BS), BF16),
            pltpu.VMEM((BS, BS), F32),
            pltpu.VMEM((ND, PER, NB, LANES), BF16),
            pltpu.VMEM((ND, PER, NB, LANES), BF16),
            pltpu.VMEM((NM, 8, LANES), BF16),
            pltpu.VMEM((NM, 8, LANES), BF16),
            pltpu.VMEM((ND * PER, NM, LANES), BF16),
            pltpu.VMEM((NM, 8, LANES), BF16),
            pltpu.VMEM((NM, 8, LANES), BF16),
            pltpu.VMEM((BS, BS), BF16),
            pltpu.VMEM((BS, BS), BF16),
            pltpu.VMEM((BS, BS), BF16),
            pltpu.VMEM((2, BS, BS), BF16),
            pltpu.VMEM((BS, BS), BF16),
            pltpu.VMEM((BS, BS), BF16),
            pltpu.VMEM((CPD, BS), F32),
            pltpu.VMEM((CPD, BS), F32),
            pltpu.VMEM((RPD, NB, CPD), BF16),
            dma((7,)),
            dma((5,)),
            dma((ND,)),
            dma((ND,)),
            dma,
            dma,
            dma((2, HALF, PER)),
            dma((2, HALF, PER)),
            dma,
            dma,
        ],
        compiler_params=pltpu.CompilerParams(collective_id=0, has_side_effects=True),
    )(
        jnp.transpose(gp[0], (1, 0, 2)),
        owner.reshape(1, NB),
        offset.reshape(1, NB),
        lf[0].T,
        rf[0].T,
        lb[0],
        rb[0],
        mom[0],
        sec[0],
    )
    upd, nlf, nrf, nmom, nsec = outs
    return (jnp.transpose(upd, (1, 0, 2)), nlf.T[None], nrf.T[None], nmom[None], nsec[None])


def solution(mesh):
    block = P("mp", None, None)
    factor = P("mp", None, "dp")
    return jax.shard_map(
        per_device,
        mesh=mesh,
        in_specs=(P("dp", None, "mp", None), P(), P(), factor, factor, block, block, block, block),
        out_specs=(P(None, "mp", "dp"), factor, factor, block, block),
        check_vma=False,
    )
```

time: 133 us -> 87.6 us (0.66)
  Pallas kernels: 0 us -> 78.8 us
  blocking collectives: 63.2 us -> 0 us
  starting transfers between devices: 28 us -> 0 us
  waiting for transfers between devices: 25.5 us -> 0 us
  local copies, waits for them, and re-layouts: 12.3 us -> 7.9 us
    pallas_call x0 -> x1, Pallas kernels: none -> 78.8 us  [per_device(): pl.pallas_call(kernel, out_shape=(jax.ShapeDtypeStruct((RPD, NB, CPD), BF...]
    all_to_all x1 -> x0, blocking collectives: 37.8 us -> none  [per_device(): lax.all_to_all(outgoing_back, 'mp', split_axis=0, concat_axis=0, tiled=True)]
    all_to_all x2 -> x0, starting transfers between devices: 28 us -> none  [the longest x1 15.7 us: per_device(): lax.all_to_all(grad_partial, 'dp', split_axis=3, concat_axis=0, tiled=True)]
    all_to_all x2 -> x0, waiting for transfers between devices: 25.5 us -> none  [the longest x1 16.7 us: per_device(): lax.all_to_all(grad_partial, 'dp', split_axis=3, concat_axis=0, tiled=True)]
    all_gather x1 -> x0, blocking collectives: 25.4 us -> none  [per_device(): arrived = lax.all_gather(landed, 'dp', axis=2, tiled=True)]
    unnamed x27 -> x7, local copies, waits for them, and re-layouts: 10.8 us -> 7.9 us
  transfers between devices with their start and end apart: 2 -> 0, of which waited for: 2 -> 0; matrix products, arithmetic and copies ran while one was open for 1% -> 0% of each run, Pallas kernels for 0% -> 0%
where the time goes in v1:
time: 87.6 us; the launch traced here: 87.3 us
  Pallas kernels  78.8 us (90%)
  local copies, waits for them, and re-layouts  7.9 us (9%)
    pallas_call x1, Pallas kernels, per_device(): pl.pallas_call(kernel, out_shape=(jax.ShapeDtypeStruct((RPD, NB, CPD), BF...  78.8 us
    unnamed x7, local copies, waits for them, and re-layouts  7.9 us

profile of v1, /device:TPU:1, one launch (start us, length us, event | category | flops | bytes accessed | tf_op | source)
XLA Modules:
  0.0 87.3 jit_solution(6687462399892133938)
XLA Ops:
  0.6 78.8 %shard_map.128 = (bf16[9,32,48]{2,1,0:T(8,128)(2,1)}, f32[48,576]{1,0:T(8,128)}, f32[48,576]{1,0:T(8,128)}, bf16[576,576]{1,0:T(8,128)(2,1)}, f32[576,576]{1,0:T(8,128)}) custom-call(bf16[9,32,576]{2,1,0:T(8,128)(2,1)} %bitcast.30, s32[1,32]{1,0:T(1,128)} %bitcast.36, s32[1,32]{1,0:T(1,128)} %bitcast.37, f32[48,576]{1,0:T(8,128)} %bitcast.31, ...), custom_call_target="tpu_custom_call" | custom-call | tf_op jit(solution)/shard_map/pallas_call | solution.py:298
  79.4 0.0 copy-start
  79.4 1.6 %copy.19 = bf16[32,9,48]{2,0,1:T(8,128)(2,1)} copy(bf16[32,9,48]{2,0,1:T(8,128)(2,1)} %bitcast.35) | data formatting | bytes 55296
  81.1 1.6 %copy.20 = f32[1,576,48]{1,2,0:T(8,128)} copy(f32[1,576,48]{1,2,0:T(8,128)} %bitcast.34) | data formatting | bytes 221184
  82.6 1.6 %copy.21 = f32[1,576,48]{1,2,0:T(8,128)} copy(f32[1,576,48]{1,2,0:T(8,128)} %bitcast.33) | data formatting | bytes 221184
  84.2 2.0 %copy.22 = bf16[1,576,576]{2,1,0:T(8,128)(2,1)} copy(bf16[1,576,576]{2,1,0:T(8,128)(2,1)} %bitcast.29) | data formatting | bytes 1327104
  86.2 0.0 copy-done
  86.2 1.1 %copy.23 = f32[1,576,576]{2,1,0:T(8,128)} copy(f32[1,576,576]{2,1,0:T(8,128)S(1)} %bitcast.25) | data formatting | bytes 2654208
Async XLA Ops:
  79.4 6.8 %copy-start = (f32[576,576]{1,0:T(8,128)S(1)}, f32[576,576]{1,0:T(8,128)}, u32[]{:S(2)}) copy-start(f32[576,576]{1,0:T(8,128)} %get-tuple-element.14) | copy-start | bytes 3981316

commit v2 on v1

v2 whole, which is shorter than its diff:
```python
import functools

import jax
import jax.numpy as jnp
from jax import lax
from jax.experimental import pallas as pl
from jax.experimental.pallas import tpu as pltpu
from jax.sharding import PartitionSpec as P

MESH = pl.DeviceIdType.MESH
F32 = jnp.float32
BF16 = jnp.bfloat16

BS = 576
NB = 32
ND = 12
NM = 64
RPD = BS // NM
CPD = BS // ND
LANES = 128
FULL = BS // LANES
REST = BS - FULL * LANES
PER = 4
HALF = ND // 2

UNITS = [((i, t),) for i in range(RPD) for t in range(FULL)]
UNITS += [tuple((i, FULL) for i in range(a, min(a + 2, RPD))) for a in range(0, RPD, 2)]
STARTS = [len(UNITS) * s // ND for s in range(ND + 1)]
SLOTS = {}
for _s in range(ND):
    for _u in range(STARTS[_s], STARTS[_s + 1]):
        for _side, _part in enumerate(UNITS[_u]):
            SLOTS[_part] = (_s * PER + _u - STARTS[_s], _side)


def _span(n, d):
    return min(d, n - d)


PEERS = sorted(
    ((dy, dx, dc) for dy in range(8) for dx in range(4) for dc in range(2) if (dy, dx, dc) != (0, 0, 0)),
    key=lambda p: (-_span(8, p[0]) - _span(4, p[1]), p),
)


def mm(a, b):
    return lax.dot_general(a, b, (((1,), (0,)), ((), ())), preferred_element_type=F32)


def mm_nt(a, b):
    return lax.dot_general(a, b, (((1,), (1,)), ((), ())), preferred_element_type=F32)


def grid2(rows, cols):
    return (
        lax.broadcasted_iota(jnp.int32, (rows, cols), 0),
        lax.broadcasted_iota(jnp.int32, (rows, cols), 1),
    )


def one_hot(mask):
    return jnp.where(mask, 1.0, 0.0).astype(BF16)


def wrap(x, n):
    return lax.rem(x, n)


def kernel(
    gp_hbm, owner_hbm, offset_hbm, lf_hbm, rf_hbm, lb_hbm, rb_hbm, mom_hbm, sec_hbm,
    land4, place, nlf, nrf, nmom, sec,
    gp, owner_ref, offset_ref, lf, rf, lb, rb, mom,
    sbuf, land1, summed, out2, land2, gu, out4,
    lbt, lbp, pre, tm, scaled, gn,
    load_sem, s1_send, s1_recv, s2_send, s2_recv, s3_send, s3_recv, s4_send, s4_recv,
):
    me_z = lax.axis_index("dp")
    me_m = lax.axis_index("mp")
    me_y, me_x, me_c = lax.div(me_m, 8), wrap(lax.div(me_m, 2), 4), wrap(me_m, 2)

    def peer(p):
        return wrap(me_y + p[0], 8) * 8 + wrap(me_x + p[1], 4) * 2 + wrap(me_c + p[2], 2)

    def has_four(s):
        n = len(UNITS)
        return lax.div((s + 1) * n, ND) - lax.div(s * n, ND) == PER

    loads = [
        pltpu.make_async_copy(src, dst, load_sem.at[i])
        for i, (src, dst) in enumerate(
            (
                (gp_hbm, gp), (owner_hbm, owner_ref), (offset_hbm, offset_ref), (lb_hbm, lb), (rb_hbm, rb),
                (mom_hbm, mom), (sec_hbm, sec), (lf_hbm, lf), (rf_hbm, rf),
            )
        )
    ]
    for copy in loads:
        copy.start()

    barrier = pltpu.get_barrier_semaphore()

    def greet_z(i, carry):
        pl.semaphore_signal(barrier, inc=1, device_id=(wrap(me_z + i, ND), me_m), device_id_type=MESH)
        return carry

    def greet_m(i, carry):
        pl.semaphore_signal(barrier, inc=1, device_id=(me_z, wrap(me_m + i, NM)), device_id_type=MESH)
        return carry

    lax.fori_loop(1, ND, greet_z, 0)
    lax.fori_loop(1, NM, greet_m, 0)

    loads[0].wait()
    for s in range(ND):
        for u in range(STARTS[s], STARTS[s + 1]):
            parts = [gp[i, :, t * LANES : min(BS, (t + 1) * LANES)] for i, t in UNITS[u]]
            if sum(p.shape[1] for p in parts) < LANES:
                parts.append(jnp.zeros((NB, LANES - parts[0].shape[1]), BF16))
            sbuf[s, u - STARTS[s]] = parts[0] if len(parts) == 1 else jnp.concatenate(parts, axis=1)

    pl.semaphore_wait(barrier, ND - 1 + NM - 1)

    def copy1(i, share, slot, to, last):
        some = pl.ds(PER - 1, 1) if last else pl.ds(0, PER - 1)
        part = 1 if last else 0
        return pltpu.make_async_remote_copy(
            src_ref=sbuf.at[share, some], dst_ref=land1.at[slot, some],
            send_sem=s1_send.at[i, part], recv_sem=s1_recv.at[slot, part],
            device_id=(to, me_m), device_id_type=MESH,
        )

    def out1(i, what):
        to = wrap(me_z + i, ND)
        what(copy1(i, to, me_z, to, False))
        pl.when(has_four(to))(lambda: what(copy1(i, to, me_z, to, True)))

    def in1(i, last):
        frm = wrap(me_z + i, ND)
        return copy1(i, me_z, frm, frm, last)

    def start(copy):
        copy.start()

    def wait_recv(copy):
        copy.wait_recv()

    def wait_send(copy):
        copy.wait_send()

    for i in [x for d in range(HALF, 0, -1) for x in sorted({d, ND - d})]:
        out1(i, start)

    loads[1].wait()
    loads[2].wait()
    owner = owner_ref[...]
    offset = offset_ref[...]
    occupied = jnp.max(jnp.where(owner == me_m, 1.0, 0.0), axis=1, keepdims=True) > 0.5
    keep_factor = jnp.where(occupied, 0.95, 1.0)
    keep_mom = jnp.where(occupied, 0.9, 1.0)
    add_factor = jnp.where(occupied, 0.05, 0.0)
    add_mom = jnp.where(occupied, 0.1, 0.0)

    row, col = grid2(NM * 8, NB)
    by_owner = one_hot(owner == row // 8)
    row, col = grid2(PER * NB, NB)
    by_offset = one_hot(offset == wrap(row, NB))
    row, col = grid2(NM * 8, PER * NB)
    route = jnp.where(wrap(row, 8) == col // NB, mm_nt(by_owner, by_offset), 0.0).astype(BF16)
    row, col = grid2(5 * NB, NB)
    at_offset = one_hot(offset == wrap(row, NB))
    row, col = grid2(5 * NB, NM * 8)
    place[...] = jnp.where(row // NB == wrap(col, 8), mm_nt(at_offset, by_owner), 0.0).astype(BF16)

    row, col = grid2(BS, BS)
    same = one_hot(row == col)
    by_slab = one_hot(col == wrap(row, NM) * RPD + row // NM)
    for copy in loads[3:]:
        copy.wait()
    lbp[...] = mm(by_slab, lb[...]).astype(BF16)
    lbt[...] = mm_nt(same, lb[...]).astype(BF16)
    tm[...] = mm(lbt[...], mom[...]).astype(BF16)
    pre[...] = mm(tm[...], rb[...])
    lbt[...] = mm_nt(same, lbp[...]).astype(BF16)

    total = [sbuf[me_z, k].astype(F32) for k in range(PER - 1)]
    near_first = [x for d in range(1, HALF + 1) for x in sorted({d, ND - d})]
    for i in near_first:
        in1(i, False).wait_recv()
        frm = wrap(me_z + i, ND)
        total = [total[k] + land1[frm, k].astype(F32) for k in range(PER - 1)]
    summed[: (PER - 1) * NB] = jnp.concatenate(total, axis=0).astype(BF16)
    summed[(PER - 1) * NB :] = jnp.zeros((NB, LANES), BF16)

    @pl.when(has_four(me_z))
    def _():
        last = sbuf[me_z, PER - 1].astype(F32)
        for i in near_first:
            in1(i, True).wait_recv()
            last = last + land1[wrap(me_z + i, ND), PER - 1].astype(F32)
        summed[(PER - 1) * NB :] = last.astype(BF16)

    out2[...] = mm(route, summed[...]).reshape(NM, 8, LANES).astype(BF16)

    def spread(src, dst, send_sem, recv_sem):
        for p in PEERS:
            to = peer(p)
            pltpu.make_async_remote_copy(
                src_ref=src.at[to], dst_ref=dst.at[me_m], send_sem=send_sem, recv_sem=recv_sem,
                device_id=(me_z, to), device_id_type=MESH,
            ).start()
        dst[me_m] = src[me_m]
        return pltpu.make_async_remote_copy(
            src_ref=src.at[pl.ds(0, NM - 1)], dst_ref=dst.at[pl.ds(0, NM - 1)], send_sem=send_sem, recv_sem=recv_sem,
            device_id=(me_z, wrap(me_m + 1, NM)), device_id_type=MESH,
        )

    done2 = spread(out2, land2, s2_send, s2_recv)
    row, col = grid2(PER * NM, NM * 8)
    gather = one_hot(col == wrap(row, NM) * 8 + row // NM)
    done2.wait_recv()
    arrived = land2[...].astype(F32).reshape(NM * 8, LANES).astype(BF16)
    gu[pl.ds(me_z * PER, PER)] = mm(gather, arrived).astype(BF16).reshape(PER, NM, LANES)

    def parent(dist):
        return (dist - 1) // 2 * 2

    def hop(way, dist, k, received):
        sign = 1 if way == 0 else -1
        origin = wrap(me_z + ND - sign * (dist if received else parent(dist)), ND)
        slot = gu.at[origin * PER + k]
        copy = pltpu.make_async_remote_copy(
            src_ref=slot, dst_ref=slot, send_sem=s3_send.at[way, dist - 1, k], recv_sem=s3_recv.at[way, dist - 1, k],
            device_id=(wrap(me_z + ND + sign * (dist - parent(dist)), ND), me_m), device_id_type=MESH,
        )
        return copy, origin

    def each(dist, received, what, ks=range(PER)):
        for k in ks:
            for way in (0, 1):
                if dist == HALF and (k < PER // 2) != (way == 0):
                    continue
                copy, origin = hop(way, dist, k, received)
                if k == PER - 1:
                    pl.when(has_four(origin))(functools.partial(what, copy))
                else:
                    what(copy)

    each(2, False, start)
    each(1, False, start)
    for dist in (2, 4):
        for k in range(PER):
            each(dist, True, wait_recv, (k,))
            each(dist + 2, False, start, (k,))
        each(dist + 1, False, start)
    for dist in (1, 3, 5, 6):
        each(dist, True, wait_recv)

    def block():
        tiles = [jnp.concatenate([gu[SLOTS[i, t][0]] for i in range(RPD)], axis=0) for t in range(FULL)]
        rest = []
        for i in range(RPD):
            slot, side = SLOTS[i, FULL]
            rest.append(gu[slot][:, side * REST : (side + 1) * REST])
        return jnp.concatenate(tiles + [jnp.concatenate(rest, axis=0)], axis=1)

    tm[...] = mm(lbt[...], block()).astype(BF16)
    step = BS // 3
    for part in range(3):
        rows = slice(part * step, (part + 1) * step)
        rotated = mm(tm[rows], rb[...])
        new_second = keep_factor * sec[rows, :] + add_factor * rotated * rotated
        sec[rows, :] = new_second
        rotated_mom = 0.9 * pre[rows, :] + 0.1 * rotated
        scaled[rows, :] = (rotated_mom / (jnp.sqrt(new_second) + 1e-08)).astype(BF16)

    unrotated = mm(lbp[...], scaled[...]).astype(BF16)
    back = rb[pl.ds(pl.multiple_of(me_z * CPD, 16), CPD), :]
    zeros = functools.partial(jnp.zeros, dtype=BF16)
    slabs = [unrotated[i * NM : (i + 1) * NM] for i in range(RPD)]
    even = mm_nt(jnp.concatenate(slabs[0::2], axis=0), jnp.concatenate([back, zeros((LANES - CPD, BS))], axis=0))
    odd = mm_nt(
        jnp.concatenate(slabs[1::2], axis=0),
        jnp.concatenate([zeros((CPD, BS)), back, zeros((LANES - 2 * CPD, BS))], axis=0),
    )
    pairs = jnp.concatenate([even[: 4 * NM] + odd, even[4 * NM :]], axis=0).astype(BF16)
    row, col = grid2(NM * 8, 5 * NM)
    out4[...] = mm(one_hot(col == wrap(row, 8) * NM + row // 8), pairs).reshape(NM, 8, LANES).astype(BF16)
    done4 = spread(out4, land4, s4_send, s4_recv)

    row, col = grid2(BS, BS)
    gn[...] = mm(one_hot(row == wrap(col, NM) * RPD + col // NM), block()).astype(BF16)
    nmom[...] = (keep_mom * mom[...].astype(F32) + add_mom * gn[...].astype(F32)).astype(BF16)
    my_rows = gn[pl.ds(pl.multiple_of(me_z * CPD, 16), CPD), :]
    nlf[...] = keep_factor * lf[...] + add_factor * mm_nt(my_rows, gn[...])
    row, col = grid2(CPD, BS)
    my_cols = mm_nt(one_hot(col == row + me_z * CPD), gn[...]).astype(BF16)
    nrf[...] = keep_factor * rf[...] + add_factor * mm(my_cols, gn[...])

    for i in range(1, ND):
        out1(i, wait_send)
    done2.wait_send()
    for dist in range(1, HALF + 1):
        each(dist, False, wait_send)
    done4.wait_send()
    done4.wait_recv()


def finish(
    land4, place, nlf, nrf, nmom, nsec,
    upd_hbm, nlf_hbm, nrf_hbm, nmom_hbm, nsec_hbm, upd, sem,
):
    copies = [
        pltpu.make_async_copy(src, dst, sem.at[i])
        for i, (src, dst) in enumerate(
            ((nsec, nsec_hbm), (nmom, nmom_hbm), (nlf, nlf_hbm), (nrf, nrf_hbm), (upd, upd_hbm))
        )
    ]
    for copy in copies[:4]:
        copy.start()
    returned = land4[...].astype(F32).reshape(NM * 8, LANES).astype(BF16)
    placed = mm(place[...], returned).astype(BF16)
    for i in range(RPD):
        pair = placed[(i // 2) * NB : (i // 2 + 1) * NB, :]
        upd[i] = pair[:, (i % 2) * CPD : (i % 2 + 1) * CPD]
    copies[4].start()
    for copy in copies:
        copy.wait()


def per_device(gp, owner, offset, lf, rf, lb, rb, mom, sec):
    hbm = pl.BlockSpec(memory_space=pltpu.HBM)
    vmem = pl.BlockSpec(memory_space=pltpu.VMEM)
    anywhere = pl.BlockSpec(memory_space=pl.ANY)
    dma = pltpu.SemaphoreType.DMA
    stay = functools.partial(pltpu.with_memory_space_constraint, memory_space=pltpu.HBM)
    inner = pl.pallas_call(
        kernel,
        out_shape=(
            pltpu.VMEM((NM, 8, LANES), BF16),
            pltpu.VMEM((5 * NB, NM * 8), BF16),
            pltpu.VMEM((CPD, BS), F32),
            pltpu.VMEM((CPD, BS), F32),
            pltpu.VMEM((BS, BS), BF16),
            pltpu.VMEM((BS, BS), F32),
        ),
        in_specs=[hbm] * 9,
        out_specs=[vmem] * 6,
        scratch_shapes=[
            pltpu.VMEM((RPD, NB, BS), BF16),
            pltpu.VMEM((1, NB), jnp.int32),
            pltpu.VMEM((1, NB), jnp.int32),
            pltpu.VMEM((CPD, BS), F32),
            pltpu.VMEM((CPD, BS), F32),
            pltpu.VMEM((BS, BS), BF16),
            pltpu.VMEM((BS, BS), BF16),
            pltpu.VMEM((BS, BS), BF16),
            pltpu.VMEM((ND, PER, NB, LANES), BF16),
            pltpu.VMEM((ND, PER, NB, LANES), BF16),
            pltpu.VMEM((PER * NB, LANES), BF16),
            pltpu.VMEM((NM, 8, LANES), BF16),
            pltpu.VMEM((NM, 8, LANES), BF16),
            pltpu.VMEM((ND * PER, NM, LANES), BF16),
            pltpu.VMEM((NM, 8, LANES), BF16),
            pltpu.VMEM((BS, BS), BF16),
            pltpu.VMEM((BS, BS), BF16),
            pltpu.VMEM((BS, BS), F32),
            pltpu.VMEM((BS, BS), BF16),
            pltpu.VMEM((BS, BS), BF16),
            pltpu.VMEM((BS, BS), BF16),
            dma((9,)),
            dma((ND, 2)),
            dma((ND, 2)),
            dma,
            dma,
            dma((2, HALF, PER)),
            dma((2, HALF, PER)),
            dma,
            dma,
        ],
        compiler_params=pltpu.CompilerParams(
            collective_id=0, has_side_effects=True, vmem_limit_bytes=40000 << 10
        ),
    )(
        stay(jnp.transpose(gp[0], (1, 0, 2))),
        stay(owner.reshape(1, NB)),
        stay(offset.reshape(1, NB)),
        stay(lf[0].T),
        stay(rf[0].T),
        stay(lb[0]),
        stay(rb[0]),
        stay(mom[0]),
        stay(sec[0]),
    )
    upd, nlf, nrf, nmom, nsec = pl.pallas_call(
        finish,
        out_shape=(
            jax.ShapeDtypeStruct((RPD, NB, CPD), BF16),
            jax.ShapeDtypeStruct((CPD, BS), F32),
            jax.ShapeDtypeStruct((CPD, BS), F32),
            jax.ShapeDtypeStruct((BS, BS), BF16),
            jax.ShapeDtypeStruct((BS, BS), F32),
        ),
        in_specs=[vmem] * 6,
        out_specs=[anywhere] * 5,
        scratch_shapes=[pltpu.VMEM((RPD, NB, CPD), BF16), dma((5,))],
        compiler_params=pltpu.CompilerParams(vmem_limit_bytes=16 << 20),
    )(*inner)
    return (jnp.transpose(upd, (1, 0, 2)), nlf.T[None], nrf.T[None], nmom[None], nsec[None])


def solution(mesh):
    block = P("mp", None, None)
    factor = P("mp", None, "dp")
    return jax.shard_map(
        per_device,
        mesh=mesh,
        in_specs=(P("dp", None, "mp", None), P(), P(), factor, factor, block, block, block, block),
        out_specs=(P(None, "mp", "dp"), factor, factor, block, block),
        check_vma=False,
    )
```

time: 87.6 us -> 67.8 us (0.77)
  Pallas kernels: 78.8 us -> 67 us
  local copies, waits for them, and re-layouts: 7.9 us -> 0 us
    pallas_call x1 -> x2, Pallas kernels: 78.8 us -> 67 us  [the longest x1 65.5 us: per_device(): pl.pallas_call(kernel, out_shape=(pltpu.VMEM((NM, 8, LANES), BF16), pltpu...]
    unnamed x7 -> x0, local copies, waits for them, and re-layouts: 7.9 us -> none
where the time goes in v2:
time: 67.8 us; the launch traced here: 67.6 us
  Pallas kernels  67 us (99%)
    pallas_call x1, Pallas kernels, per_device(): pl.pallas_call(kernel, out_shape=(pltpu.VMEM((NM, 8, LANES), BF16), pltpu...  65.5 us
    pallas_call x1, Pallas kernels, per_device(): pl.pallas_call(finish, out_shape=(jax.ShapeDtypeStruct((RPD, NB, CPD), BF...  1.49 us

profile of v2, /device:TPU:1, one launch (start us, length us, event | category | flops | bytes accessed | tf_op | source)
XLA Modules:
  0.0 67.6 jit_solution(1696194621408173229)
XLA Ops:
  0.6 65.5 %shard_map.128 = (bf16[64,8,128]{2,1,0:T(8,128)(2,1)S(1)}, bf16[160,512]{1,0:T(8,128)(2,1)S(1)}, f32[48,576]{1,0:T(8,128)S(1)}, f32[48,576]{1,0:T(8,128)S(1)}, b...) custom-call(bf16[9,32,576]{2,1,0:T(8,128)(2,1)} %bitcast.28, s32[1,32]{1,0:T(1,128)} %bitcast.31, s32[1,32]{1,0:T(1,128)} %bitcast.32, ...), custom_call_target="tpu_custom_call" | custom-call | tf_op jit(solution)/shard_map/pallas_call | solution.py:336
  66.2 1.5 %shard_map.129 = (bf16[9,32,48]{2,1,0:T(8,128)(2,1)}, f32[48,576]{1,0:T(8,128)}, f32[48,576]{1,0:T(8,128)}, bf16[576,576]{1,0:T(8,128)(2,1)}, f32[576,576]{1,0:T(8,128)}) custom-call(bf16[64,8,128]{2,1,0:T(8,128)(2,1)S(1)} %get-tuple-element.16.land4, bf16[160,512]{1,0:T(8,128)(2,1)S(1)} %get-tuple-element.17.place, f32[48,576]{1,0:T(8,128)S(1)} %get-tuple-element.18.nlf, ...), custom_call_target="tpu_custom_call" | custom-call | tf_op jit(solution)/shard_map/pallas_call | solution.py:394

commit v3 on v2

v3 whole, which is shorter than its diff:
```python
import functools

import jax
import jax.numpy as jnp
from jax import lax
from jax.experimental import pallas as pl
from jax.experimental.pallas import tpu as pltpu
from jax.sharding import PartitionSpec as P

MESH = pl.DeviceIdType.MESH
F32 = jnp.float32
BF16 = jnp.bfloat16

BS = 576
NB = 32
ND = 12
NM = 64
NY = 8
NQ = NM // NY
AWAY = (0, 2, ND - 2, 1, ND - 1)
RPD = BS // NM
CPD = BS // ND
LANES = 128
FULL = BS // LANES
REST = BS - FULL * LANES
PER = 4
HALF = ND // 2

UNITS = [((i, t),) for i in range(RPD) for t in range(FULL)]
UNITS += [tuple((i, FULL) for i in range(a, min(a + 2, RPD))) for a in range(0, RPD, 2)]
STARTS = [len(UNITS) * s // ND for s in range(ND + 1)]
SLOTS = {}
for _s in range(ND):
    for _u in range(STARTS[_s], STARTS[_s + 1]):
        for _side, _part in enumerate(UNITS[_u]):
            SLOTS[_part] = (_s * PER + _u - STARTS[_s], _side)


def _span(n, d):
    return min(d, n - d)


PEERS = sorted(
    ((dy, dx, dc) for dy in range(8) for dx in range(4) for dc in range(2) if (dy, dx, dc) != (0, 0, 0)),
    key=lambda p: (-_span(8, p[0]) - _span(4, p[1]), p),
)


def mm(a, b):
    return lax.dot_general(a, b, (((1,), (0,)), ((), ())), preferred_element_type=F32)


def mm_nt(a, b):
    return lax.dot_general(a, b, (((1,), (1,)), ((), ())), preferred_element_type=F32)


def grid2(rows, cols):
    return (
        lax.broadcasted_iota(jnp.int32, (rows, cols), 0),
        lax.broadcasted_iota(jnp.int32, (rows, cols), 1),
    )


def one_hot(mask):
    return jnp.where(mask, 1.0, 0.0).astype(BF16)


def wrap(x, n):
    return lax.rem(x, n)


def kernel(
    gp_hbm, owner_hbm, offset_hbm, lf_hbm, rf_hbm, lb_hbm, rb_hbm, mom_hbm, sec_hbm,
    land4, place, nlf, nrf, nmom, sec,
    gp, owner_ref, offset_ref, lf, rf, lb, rb, mom,
    sbuf, land1, agg, summed, out2, land2, out3, land3, gu, out4,
    route, turn, gather, lbt, lbp, pre, tm, scaled, gn,
    load_sem, s1_send, s1_recv, s2_send, s2_recv, s3_send, s3_recv, s4_send, s4_recv, s5_send, s5_recv,
):
    me_z = lax.axis_index("dp")
    me_m = lax.axis_index("mp")
    me_y, me_x, me_c = lax.div(me_m, 8), wrap(lax.div(me_m, 2), 4), wrap(me_m, 2)

    def peer(p):
        return wrap(me_y + p[0], 8) * 8 + wrap(me_x + p[1], 4) * 2 + wrap(me_c + p[2], 2)

    def has_four(s):
        n = len(UNITS)
        return lax.div((s + 1) * n, ND) - lax.div(s * n, ND) == PER

    loads = [
        pltpu.make_async_copy(src, dst, load_sem.at[i])
        for i, (src, dst) in enumerate(
            (
                (gp_hbm, gp), (owner_hbm, owner_ref), (offset_hbm, offset_ref), (lb_hbm, lb), (rb_hbm, rb),
                (mom_hbm, mom), (sec_hbm, sec), (lf_hbm, lf), (rf_hbm, rf),
            )
        )
    ]
    for copy in loads:
        copy.start()

    barrier = pltpu.get_barrier_semaphore()

    me_q = wrap(me_m, NQ)

    def at(dz, dy, dq):
        return (wrap(me_z + dz, ND), wrap(me_y + dy, NY) * NQ + wrap(me_q + dq, NQ))

    def greet(dz, dy, dq):
        pl.semaphore_signal(barrier, inc=1, device_id=at(dz, dy, dq), device_id_type=MESH)

    def greet_y(i, carry):
        greet(0, i, 0)
        return carry

    def greet_q(dz, i, carry):
        greet(dz, 0, i)
        return carry

    for dz in AWAY[1:] + AWAY[:1]:
        lax.fori_loop(0 if dz else 1, NQ, functools.partial(greet_q, dz), 0)
    lax.fori_loop(1, NY, greet_y, 0)

    loads[0].wait()
    for s in range(ND):
        for u in range(STARTS[s], STARTS[s + 1]):
            parts = [gp[i, :, t * LANES : min(BS, (t + 1) * LANES)] for i, t in UNITS[u]]
            if sum(p.shape[1] for p in parts) < LANES:
                parts.append(jnp.zeros((NB, LANES - parts[0].shape[1]), BF16))
            sbuf[s, u - STARTS[s]] = parts[0] if len(parts) == 1 else jnp.concatenate(parts, axis=1)

    pl.semaphore_wait(barrier, len(AWAY) * NQ - 1 + NY - 1)

    def parent(dist):
        return (dist - 1) // 2 * 2

    def hop1(way, dist, part, received):
        sign = 1 if way == 0 else -1
        share = wrap(me_z + ND + sign * (parent(dist) if received else dist), ND)
        if dist == HALF:
            a, n = ((0, 2), None)[part] if way == 0 else ((2, 1), (3, 1))[part]
        else:
            a, n = ((0, PER - 1), (PER - 1, 1))[part]
        some = pl.ds(a, n)
        if dist in (2, 4):
            src = agg.at[way, dist // 2 - 1, some]
        else:
            src = sbuf.at[share, some]
        copy = pltpu.make_async_remote_copy(
            src_ref=src, dst_ref=land1.at[way, dist - 1, some],
            send_sem=s1_send.at[way, dist - 1, part], recv_sem=s1_recv.at[way, dist - 1, part],
            device_id=(wrap(me_z + ND + sign * (dist - parent(dist)), ND), me_m), device_id_type=MESH,
        )
        return copy, share

    def each1(dist, received, what):
        for way in (0, 1):
            what(hop1(way, dist, 0, received)[0])
            if dist == HALF and way == 0:
                continue
            copy, share = hop1(way, dist, 1, received)
            pl.when(has_four(share))(functools.partial(what, copy))

    def start(copy):
        copy.start()

    def wait_recv(copy):
        copy.wait_recv()

    def wait_send(copy):
        copy.wait_send()

    def relay(dist):
        each1(dist + 1, True, wait_recv)
        each1(dist + 2, True, wait_recv)
        for way in (0, 1):
            share = wrap(me_z + ND + (dist if way == 0 else -dist), ND)
            for k in range(PER):
                behind = [dist + 1]
                if dist + 2 < HALF or (k < PER // 2) == (way == 0):
                    behind.append(dist + 2)

                def add(k=k, way=way, share=share, behind=behind):
                    total = sbuf[share, k].astype(F32)
                    for d in behind:
                        total = total + land1[way, d - 1, k].astype(F32)
                    agg[way, dist // 2 - 1, k] = total.astype(BF16)

                if k == PER - 1:
                    pl.when(has_four(share))(add)
                else:
                    add()
        each1(dist, False, start)

    for dist in (6, 5, 3, 1):
        each1(dist, False, start)

    loads[1].wait()
    loads[2].wait()
    owner = owner_ref[...]
    offset = offset_ref[...]
    occupied = jnp.max(jnp.where(owner == me_m, 1.0, 0.0), axis=1, keepdims=True) > 0.5
    keep_factor = jnp.where(occupied, 0.95, 1.0)
    keep_mom = jnp.where(occupied, 0.9, 1.0)
    add_factor = jnp.where(occupied, 0.05, 0.0)
    add_mom = jnp.where(occupied, 0.1, 0.0)

    row, col = grid2(NM * PER, NB)
    by_owner = one_hot(owner == row // PER)
    row, col = grid2(PER * NB, NB)
    by_offset = one_hot(offset == wrap(row, NB))
    row, col = grid2(NM * PER, PER * NB)
    route[...] = jnp.where(wrap(row, PER) == col // NB, mm_nt(by_owner, by_offset), 0.0).astype(BF16)
    row, col = grid2(NM * PER, NM * PER)
    line = NY * PER
    turn[...] = one_hot(col == wrap(row, line) // PER * line + row // line * PER + wrap(row, PER))
    gather[...] = one_hot(col == wrap(row, NQ) * line + wrap(row, NM) // NQ * PER + row // NM)
    row, col = grid2(NM * 8, NB)
    by_owner = one_hot(owner == row // 8)
    row, col = grid2(5 * NB, NB)
    at_offset = one_hot(offset == wrap(row, NB))
    row, col = grid2(5 * NB, NM * 8)
    place[...] = jnp.where(row // NB == wrap(col, 8), mm_nt(at_offset, by_owner), 0.0).astype(BF16)
    row, col = grid2(BS, BS)
    for copy in loads[3:]:
        copy.wait()
    lbp[...] = mm(one_hot(col == wrap(row, NM) * RPD + row // NM), lb[...]).astype(BF16)

    relay(4)

    row, col = grid2(BS, BS)
    same = one_hot(row == col)
    lbt[...] = mm_nt(same, lb[...]).astype(BF16)
    tm[...] = mm(lbt[...], mom[...]).astype(BF16)

    relay(2)

    pre[...] = mm(tm[...], rb[...])
    lbt[...] = mm_nt(same, lbp[...]).astype(BF16)

    each1(1, True, wait_recv)
    each1(2, True, wait_recv)

    def add_up(k):
        total = sbuf[me_z, k].astype(F32)
        for way in (0, 1):
            for d in (1, 2):
                total = total + land1[way, d - 1, k].astype(F32)
        summed[k * NB : (k + 1) * NB] = total.astype(BF16)

    for k in range(PER - 1):
        add_up(k)
    summed[(PER - 1) * NB :] = jnp.zeros((NB, LANES), BF16)
    pl.when(has_four(me_z))(functools.partial(add_up, PER - 1))

    lines = mm(route[...], summed[...]).reshape(NY, line, LANES).astype(BF16)
    out2[...] = lines

    def to_line(dy):
        return pltpu.make_async_remote_copy(
            src_ref=out2.at[wrap(me_y + dy, NY)], dst_ref=land2.at[me_y], send_sem=s2_send, recv_sem=s2_recv,
            device_id=at(0, dy, 0), device_id_type=MESH,
        )

    for dy in (4, 3, 5, 2, 6, 1, 7):
        to_line(dy).start()
    land2[me_y] = out2[me_y]
    done2 = pltpu.make_async_remote_copy(
        src_ref=out2.at[pl.ds(0, NY - 1)], dst_ref=land2.at[pl.ds(0, NY - 1)], send_sem=s2_send, recv_sem=s2_recv,
        device_id=at(0, 1, 0), device_id_type=MESH,
    )
    done2.wait_recv()
    out3[...] = mm(turn[...], land2[...].reshape(NM * PER, LANES)).reshape(NQ, line, LANES).astype(BF16)

    def to_owner(n, dq):
        return pltpu.make_async_remote_copy(
            src_ref=out3.at[wrap(me_q + dq, NQ)], dst_ref=land3.at[n, me_q], send_sem=s5_send.at[n], recv_sem=s5_recv.at[n],
            device_id=at(AWAY[n], 0, dq), device_id_type=MESH,
        )

    for n in (1, 2, 3, 4, 0):
        for dq in (4, 5, 3, 2, 6, 7, 1, 0):
            if n or dq:
                to_owner(n, dq).start()
    land3[0, me_q] = out3[me_q]

    def all_rows(n):
        some = pl.ds(0, NQ if n else NQ - 1)
        return pltpu.make_async_remote_copy(
            src_ref=out3.at[some], dst_ref=land3.at[n, some], send_sem=s5_send.at[n], recv_sem=s5_recv.at[n],
            device_id=at(AWAY[n], 0, 1), device_id_type=MESH,
        )

    def take(n):
        all_rows(n).wait_recv()
        share = mm(gather[...], land3[n].reshape(NM * PER, LANES)).astype(BF16)
        gu[pl.ds(wrap(me_z + ND - AWAY[n], ND) * PER, PER)] = share.reshape(PER, NM, LANES)

    def hop(way, dist, k, received):
        sign = 1 if way == 0 else -1
        origin = wrap(me_z + ND - sign * (dist if received else parent(dist)), ND)
        slot = gu.at[origin * PER + k]
        copy = pltpu.make_async_remote_copy(
            src_ref=slot, dst_ref=slot, send_sem=s3_send.at[way, dist - 1, k], recv_sem=s3_recv.at[way, dist - 1, k],
            device_id=(wrap(me_z + ND + sign * (dist - parent(dist)), ND), me_m), device_id_type=MESH,
        )
        return copy, origin

    def each(dist, received, what, ks=range(PER), ways=(0, 1)):
        for k in ks:
            for way in ways:
                if dist == HALF and (k < PER // 2) != (way == 0):
                    continue
                copy, origin = hop(way, dist, k, received)
                if k == PER - 1:
                    pl.when(has_four(origin))(functools.partial(what, copy))
                else:
                    what(copy)

    take(1)
    each(4, False, start, ways=(0,))
    take(2)
    each(4, False, start, ways=(1,))
    each(3, False, start)
    take(3)
    take(4)
    take(0)
    for k in range(PER):
        each(4, True, wait_recv, (k,))
        each(6, False, start, (k,))
    each(5, False, start)
    for dist in (3, 5, 6):
        each(dist, True, wait_recv)

    def block():
        tiles = [jnp.concatenate([gu[SLOTS[i, t][0]] for i in range(RPD)], axis=0) for t in range(FULL)]
        rest = []
        for i in range(RPD):
            slot, side = SLOTS[i, FULL]
            rest.append(gu[slot][:, side * REST : (side + 1) * REST])
        return jnp.concatenate(tiles + [jnp.concatenate(rest, axis=0)], axis=1)

    tm[...] = mm(lbt[...], block()).astype(BF16)
    step = BS // 3
    for part in range(3):
        rows = slice(part * step, (part + 1) * step)
        rotated = mm(tm[rows], rb[...])
        new_second = keep_factor * sec[rows, :] + add_factor * rotated * rotated
        sec[rows, :] = new_second
        rotated_mom = 0.9 * pre[rows, :] + 0.1 * rotated
        scaled[rows, :] = (rotated_mom / (jnp.sqrt(new_second) + 1e-08)).astype(BF16)

    back = rb[pl.ds(pl.multiple_of(me_z * CPD, 16), CPD), :]
    zeros = functools.partial(jnp.zeros, dtype=BF16)
    twice = jnp.concatenate([back, back, zeros((LANES - 2 * CPD, BS))], axis=0)
    turned_back = mm(lbp[...], mm_nt(scaled[...], twice).astype(BF16))
    slabs = [turned_back[i * NM : (i + 1) * NM] for i in range(RPD)]
    lane = lax.broadcasted_iota(jnp.int32, (NM, LANES), 1)
    pairs = [jnp.where(lane < CPD, slabs[i], slabs[min(i + 1, RPD - 1)]) for i in range(0, RPD, 2)]
    pairs = jnp.concatenate(pairs, axis=0).astype(BF16)
    row, col = grid2(NM * 8, 5 * NM)
    out4[...] = mm(one_hot(col == wrap(row, 8) * NM + row // 8), pairs).reshape(NM, 8, LANES).astype(BF16)
    def spread(src, dst, send_sem, recv_sem):
        for p in PEERS:
            to = peer(p)
            pltpu.make_async_remote_copy(
                src_ref=src.at[to], dst_ref=dst.at[me_m], send_sem=send_sem, recv_sem=recv_sem,
                device_id=(me_z, to), device_id_type=MESH,
            ).start()
        dst[me_m] = src[me_m]
        return pltpu.make_async_remote_copy(
            src_ref=src.at[pl.ds(0, NM - 1)], dst_ref=dst.at[pl.ds(0, NM - 1)], send_sem=send_sem, recv_sem=recv_sem,
            device_id=(me_z, wrap(me_m + 1, NM)), device_id_type=MESH,
        )

    done4 = spread(out4, land4, s4_send, s4_recv)

    row, col = grid2(BS, BS)
    gn[...] = mm(one_hot(row == wrap(col, NM) * RPD + col // NM), block()).astype(BF16)
    nmom[...] = (keep_mom * mom[...].astype(F32) + add_mom * gn[...].astype(F32)).astype(BF16)
    my_rows = gn[pl.ds(pl.multiple_of(me_z * CPD, 16), CPD), :]
    nlf[...] = keep_factor * lf[...] + add_factor * mm_nt(my_rows, gn[...])
    row, col = grid2(CPD, BS)
    my_cols = mm_nt(one_hot(col == row + me_z * CPD), gn[...]).astype(BF16)
    nrf[...] = keep_factor * rf[...] + add_factor * mm(my_cols, gn[...])

    for dist in range(1, HALF + 1):
        each1(dist, False, wait_send)
    done2.wait_send()
    for n in range(len(AWAY)):
        all_rows(n).wait_send()
    for dist in range(3, HALF + 1):
        each(dist, False, wait_send)
    done4.wait_send()
    done4.wait_recv()


def finish(
    land4, place, nlf, nrf, nmom, nsec,
    upd_hbm, nlf_hbm, nrf_hbm, nmom_hbm, nsec_hbm, upd, sem,
):
    copies = [
        pltpu.make_async_copy(src, dst, sem.at[i])
        for i, (src, dst) in enumerate(
            ((nsec, nsec_hbm), (nmom, nmom_hbm), (nlf, nlf_hbm), (nrf, nrf_hbm), (upd, upd_hbm))
        )
    ]
    for copy in copies[:4]:
        copy.start()
    returned = land4[...].astype(F32).reshape(NM * 8, LANES).astype(BF16)
    placed = mm(place[...], returned).astype(BF16)
    for i in range(RPD):
        pair = placed[(i // 2) * NB : (i // 2 + 1) * NB, :]
        upd[i] = pair[:, (i % 2) * CPD : (i % 2 + 1) * CPD]
    copies[4].start()
    for copy in copies:
        copy.wait()


def per_device(gp, owner, offset, lf, rf, lb, rb, mom, sec):
    hbm = pl.BlockSpec(memory_space=pltpu.HBM)
    vmem = pl.BlockSpec(memory_space=pltpu.VMEM)
    anywhere = pl.BlockSpec(memory_space=pl.ANY)
    dma = pltpu.SemaphoreType.DMA
    stay = functools.partial(pltpu.with_memory_space_constraint, memory_space=pltpu.HBM)
    inner = pl.pallas_call(
        kernel,
        out_shape=(
            pltpu.VMEM((NM, 8, LANES), BF16),
            pltpu.VMEM((5 * NB, NM * 8), BF16),
            pltpu.VMEM((CPD, BS), F32),
            pltpu.VMEM((CPD, BS), F32),
            pltpu.VMEM((BS, BS), BF16),
            pltpu.VMEM((BS, BS), F32),
        ),
        in_specs=[hbm] * 9,
        out_specs=[vmem] * 6,
        scratch_shapes=[
            pltpu.VMEM((RPD, NB, BS), BF16),
            pltpu.VMEM((1, NB), jnp.int32),
            pltpu.VMEM((1, NB), jnp.int32),
            pltpu.VMEM((CPD, BS), F32),
            pltpu.VMEM((CPD, BS), F32),
            pltpu.VMEM((BS, BS), BF16),
            pltpu.VMEM((BS, BS), BF16),
            pltpu.VMEM((BS, BS), BF16),
            pltpu.VMEM((ND, PER, NB, LANES), BF16),
            pltpu.VMEM((2, HALF, PER, NB, LANES), BF16),
            pltpu.VMEM((2, 2, PER, NB, LANES), BF16),
            pltpu.VMEM((PER * NB, LANES), BF16),
            pltpu.VMEM((NY, NQ * PER, LANES), BF16),
            pltpu.VMEM((NY, NQ * PER, LANES), BF16),
            pltpu.VMEM((NQ, NY * PER, LANES), BF16),
            pltpu.VMEM((len(AWAY), NQ, NY * PER, LANES), BF16),
            pltpu.VMEM((ND * PER, NM, LANES), BF16),
            pltpu.VMEM((NM, 8, LANES), BF16),
            pltpu.VMEM((NM * PER, PER * NB), BF16),
            pltpu.VMEM((NM * PER, NM * PER), BF16),
            pltpu.VMEM((NM * PER, NM * PER), BF16),
            pltpu.VMEM((BS, BS), BF16),
            pltpu.VMEM((BS, BS), BF16),
            pltpu.VMEM((BS, BS), F32),
            pltpu.VMEM((BS, BS), BF16),
            pltpu.VMEM((BS, BS), BF16),
            pltpu.VMEM((BS, BS), BF16),
            dma((9,)),
            dma((2, HALF, 2)),
            dma((2, HALF, 2)),
            dma,
            dma,
            dma((2, HALF, PER)),
            dma((2, HALF, PER)),
            dma,
            dma,
            dma((len(AWAY),)),
            dma((len(AWAY),)),
        ],
        compiler_params=pltpu.CompilerParams(
            collective_id=0, has_side_effects=True, vmem_limit_bytes=40000 << 10
        ),
    )(
        stay(jnp.transpose(gp[0], (1, 0, 2))),
        stay(owner.reshape(1, NB)),
        stay(offset.reshape(1, NB)),
        stay(lf[0].T),
        stay(rf[0].T),
        stay(lb[0]),
        stay(rb[0]),
        stay(mom[0]),
        stay(sec[0]),
    )
    upd, nlf, nrf, nmom, nsec = pl.pallas_call(
        finish,
        out_shape=(
            jax.ShapeDtypeStruct((RPD, NB, CPD), BF16),
            jax.ShapeDtypeStruct((CPD, BS), F32),
            jax.ShapeDtypeStruct((CPD, BS), F32),
            jax.ShapeDtypeStruct((BS, BS), BF16),
            jax.ShapeDtypeStruct((BS, BS), F32),
        ),
        in_specs=[vmem] * 6,
        out_specs=[anywhere] * 5,
        scratch_shapes=[pltpu.VMEM((RPD, NB, CPD), BF16), dma((5,))],
        compiler_params=pltpu.CompilerParams(vmem_limit_bytes=16 << 20),
    )(*inner)
    return (jnp.transpose(upd, (1, 0, 2)), nlf.T[None], nrf.T[None], nmom[None], nsec[None])


def solution(mesh):
    block = P("mp", None, None)
    factor = P("mp", None, "dp")
    return jax.shard_map(
        per_device,
        mesh=mesh,
        in_specs=(P("dp", None, "mp", None), P(), P(), factor, factor, block, block, block, block),
        out_specs=(P(None, "mp", "dp"), factor, factor, block, block),
        check_vma=False,
    )
```

time: 67.8 us -> 64 us (0.944)
  Pallas kernels: 67 us -> 63.2 us
    pallas_call x1, Pallas kernels: 65.5 us -> 61.7 us  [per_device(): pl.pallas_call(kernel, out_shape=(pltpu.VMEM((NM, 8, LANES), BF16), pltpu...]
where the time goes in v3:
time: 64 us; the launch traced here: 63.9 us
  Pallas kernels  63.2 us (99%)
  between operations  0.64 us (1%)
    pallas_call x1, Pallas kernels, per_device(): pl.pallas_call(kernel, out_shape=(pltpu.VMEM((NM, 8, LANES), BF16), pltpu...  61.7 us
    pallas_call x1, Pallas kernels, per_device(): pl.pallas_call(finish, out_shape=(jax.ShapeDtypeStruct((RPD, NB, CPD), BF...  1.49 us

profile of v3, /device:TPU:1, one launch (start us, length us, event | category | flops | bytes accessed | tf_op | source)
XLA Modules:
  0.0 63.9 jit_solution(18325612891382249387)
XLA Ops:
  0.6 61.7 %shard_map.128 = (bf16[64,8,128]{2,1,0:T(8,128)(2,1)S(1)}, bf16[160,512]{1,0:T(8,128)(2,1)S(1)}, f32[48,576]{1,0:T(8,128)S(1)}, f32[48,576]{1,0:T(8,128)S(1)}, b...) custom-call(bf16[9,32,576]{2,1,0:T(8,128)(2,1)} %bitcast.28, s32[1,32]{1,0:T(1,128)} %bitcast.31, s32[1,32]{1,0:T(1,128)} %bitcast.32, ...), custom_call_target="tpu_custom_call" | custom-call | tf_op jit(solution)/shard_map/pallas_call | solution.py:427
  62.4 1.5 %shard_map.129 = (bf16[9,32,48]{2,1,0:T(8,128)(2,1)}, f32[48,576]{1,0:T(8,128)}, f32[48,576]{1,0:T(8,128)}, bf16[576,576]{1,0:T(8,128)(2,1)}, f32[576,576]{1,0:T(8,128)}) custom-call(bf16[64,8,128]{2,1,0:T(8,128)(2,1)S(1)} %get-tuple-element.16.land4, bf16[160,512]{1,0:T(8,128)(2,1)S(1)} %get-tuple-element.17.place, f32[48,576]{1,0:T(8,128)S(1)} %get-tuple-element.18.nlf, ...), custom_call_target="tpu_custom_call" | custom-call | tf_op jit(solution)/shard_map/pallas_call | solution.py:493

commit v4 on v3

--- a/solution.py
+++ b/solution.py
@@ -56,8 +56,8 @@
 
 def grid2(rows, cols):
     return (
-        lax.broadcasted_iota(jnp.int32, (rows, cols), 0),
-        lax.broadcasted_iota(jnp.int32, (rows, cols), 1),
+        lax.broadcasted_iota(jnp.int32, (rows, 1), 0),
+        lax.broadcasted_iota(jnp.int32, (1, cols), 1),
     )
 
 
@@ -67,6 +67,19 @@
 
 def wrap(x, n):
     return lax.rem(x, n)
+
+
+def roll(x, lanes):
+    return pltpu.roll(x, lanes % LANES, 1) if lanes % LANES else x
+
+
+def pieces(q):
+    where = []
+    for i in range(RPD):
+        lo, hi = max(i * CPD, q * LANES), min((i + 1) * CPD, (q + 1) * LANES)
+        if lo < hi:
+            where.append((i, lo - q * LANES, hi - q * LANES))
+    return where
 
 
 def kernel(
@@ -81,12 +94,22 @@
     me_m = lax.axis_index("mp")
     me_y, me_x, me_c = lax.div(me_m, 8), wrap(lax.div(me_m, 2), 4), wrap(me_m, 2)
 
+    me_q = wrap(me_m, NQ)
+    zs = [wrap(me_z + d, ND) for d in range(ND)]
+    ys = [wrap(me_y + d, NY) for d in range(NY)]
+    rows_y = [y * NQ for y in ys]
+    qs = [wrap(me_q + d, NQ) for d in range(NQ)]
+    xs = [wrap(me_x + d, 4) * 2 for d in range(4)]
+    cs = [wrap(me_c + d, 2) for d in range(2)]
+
     def peer(p):
-        return wrap(me_y + p[0], 8) * 8 + wrap(me_x + p[1], 4) * 2 + wrap(me_c + p[2], 2)
-
-    def has_four(s):
-        n = len(UNITS)
-        return lax.div((s + 1) * n, ND) - lax.div(s * n, ND) == PER
+        return rows_y[p[0]] + xs[p[1]] + cs[p[2]]
+
+    ends = [lax.div((z + 1) * len(UNITS), ND) - lax.div(z * len(UNITS), ND) for z in zs]
+    fours = [n == PER for n in ends]
+
+    def has_four(off):
+        return fours[off % ND]
 
     loads = [
         pltpu.make_async_copy(src, dst, load_sem.at[i])
@@ -97,30 +120,22 @@
             )
         )
     ]
-    for copy in loads:
-        copy.start()
+    loads[0].start()
 
     barrier = pltpu.get_barrier_semaphore()
 
-    me_q = wrap(me_m, NQ)
-
     def at(dz, dy, dq):
-        return (wrap(me_z + dz, ND), wrap(me_y + dy, NY) * NQ + wrap(me_q + dq, NQ))
+        return (zs[dz % ND], rows_y[dy] + qs[dq])
 
     def greet(dz, dy, dq):
         pl.semaphore_signal(barrier, inc=1, device_id=at(dz, dy, dq), device_id_type=MESH)
 
-    def greet_y(i, carry):
-        greet(0, i, 0)
-        return carry
-
-    def greet_q(dz, i, carry):
-        greet(dz, 0, i)
-        return carry
-
+    for dy in (4, 3, 5, 2, 6, 1, 7):
+        greet(0, dy, 0)
     for dz in AWAY[1:] + AWAY[:1]:
-        lax.fori_loop(0 if dz else 1, NQ, functools.partial(greet_q, dz), 0)
-    lax.fori_loop(1, NY, greet_y, 0)
+        for dq in (4, 5, 3, 2, 6, 7, 1, 0):
+            if dz or dq:
+                greet(dz, 0, dq)
 
     loads[0].wait()
     for s in range(ND):
@@ -130,6 +145,8 @@
                 parts.append(jnp.zeros((NB, LANES - parts[0].shape[1]), BF16))
             sbuf[s, u - STARTS[s]] = parts[0] if len(parts) == 1 else jnp.concatenate(parts, axis=1)
 
+    for copy in loads[1:]:
+        copy.start()
     pl.semaphore_wait(barrier, len(AWAY) * NQ - 1 + NY - 1)
 
     def parent(dist):
@@ -137,7 +154,8 @@
 
     def hop1(way, dist, part, received):
         sign = 1 if way == 0 else -1
-        share = wrap(me_z + ND + sign * (parent(dist) if received else dist), ND)
+        off = sign * (parent(dist) if received else dist)
+        share = zs[off % ND]
         if dist == HALF:
             a, n = ((0, 2), None)[part] if way == 0 else ((2, 1), (3, 1))[part]
         else:
@@ -150,17 +168,17 @@
         copy = pltpu.make_async_remote_copy(
             src_ref=src, dst_ref=land1.at[way, dist - 1, some],
             send_sem=s1_send.at[way, dist - 1, part], recv_sem=s1_recv.at[way, dist - 1, part],
-            device_id=(wrap(me_z + ND + sign * (dist - parent(dist)), ND), me_m), device_id_type=MESH,
-        )
-        return copy, share
+            device_id=(zs[sign * (dist - parent(dist)) % ND], me_m), device_id_type=MESH,
+        )
+        return copy, off
 
     def each1(dist, received, what):
         for way in (0, 1):
             what(hop1(way, dist, 0, received)[0])
             if dist == HALF and way == 0:
                 continue
-            copy, share = hop1(way, dist, 1, received)
-            pl.when(has_four(share))(functools.partial(what, copy))
+            copy, off = hop1(way, dist, 1, received)
+            pl.when(has_four(off))(functools.partial(what, copy))
 
     def start(copy):
         copy.start()
@@ -175,7 +193,8 @@
         each1(dist + 1, True, wait_recv)
         each1(dist + 2, True, wait_recv)
         for way in (0, 1):
-            share = wrap(me_z + ND + (dist if way == 0 else -dist), ND)
+            off = dist if way == 0 else -dist
+            share = zs[off % ND]
             for k in range(PER):
                 behind = [dist + 1]
                 if dist + 2 < HALF or (k < PER // 2) == (way == 0):
@@ -188,7 +207,7 @@
                     agg[way, dist // 2 - 1, k] = total.astype(BF16)
 
                 if k == PER - 1:
-                    pl.when(has_four(share))(add)
+                    pl.when(has_four(off))(add)
                 else:
                     add()
         each1(dist, False, start)
@@ -212,16 +231,6 @@
     by_offset = one_hot(offset == wrap(row, NB))
     row, col = grid2(NM * PER, PER * NB)
     route[...] = jnp.where(wrap(row, PER) == col // NB, mm_nt(by_owner, by_offset), 0.0).astype(BF16)
-    row, col = grid2(NM * PER, NM * PER)
-    line = NY * PER
-    turn[...] = one_hot(col == wrap(row, line) // PER * line + row // line * PER + wrap(row, PER))
-    gather[...] = one_hot(col == wrap(row, NQ) * line + wrap(row, NM) // NQ * PER + row // NM)
-    row, col = grid2(NM * 8, NB)
-    by_owner = one_hot(owner == row // 8)
-    row, col = grid2(5 * NB, NB)
-    at_offset = one_hot(offset == wrap(row, NB))
-    row, col = grid2(5 * NB, NM * 8)
-    place[...] = jnp.where(row // NB == wrap(col, 8), mm_nt(at_offset, by_owner), 0.0).astype(BF16)
     row, col = grid2(BS, BS)
     for copy in loads[3:]:
         copy.wait()
@@ -252,14 +261,15 @@
     for k in range(PER - 1):
         add_up(k)
     summed[(PER - 1) * NB :] = jnp.zeros((NB, LANES), BF16)
-    pl.when(has_four(me_z))(functools.partial(add_up, PER - 1))
-
+    pl.when(has_four(0))(functools.partial(add_up, PER - 1))
+
+    line = NY * PER
     lines = mm(route[...], summed[...]).reshape(NY, line, LANES).astype(BF16)
     out2[...] = lines
 
     def to_line(dy):
         return pltpu.make_async_remote_copy(
-            src_ref=out2.at[wrap(me_y + dy, NY)], dst_ref=land2.at[me_y], send_sem=s2_send, recv_sem=s2_recv,
+            src_ref=out2.at[ys[dy]], dst_ref=land2.at[me_y], send_sem=s2_send, recv_sem=s2_recv,
             device_id=at(0, dy, 0), device_id_type=MESH,
         )
 
@@ -270,12 +280,15 @@
         src_ref=out2.at[pl.ds(0, NY - 1)], dst_ref=land2.at[pl.ds(0, NY - 1)], send_sem=s2_send, recv_sem=s2_recv,
         device_id=at(0, 1, 0), device_id_type=MESH,
     )
+    row, col = grid2(NM * PER, NM * PER)
+    turn[...] = one_hot(col == wrap(row, line) // PER * line + row // line * PER + wrap(row, PER))
+    gather[...] = one_hot(col == wrap(row, NQ) * line + wrap(row, NM) // NQ * PER + row // NM)
     done2.wait_recv()
     out3[...] = mm(turn[...], land2[...].reshape(NM * PER, LANES)).reshape(NQ, line, LANES).astype(BF16)
 
     def to_owner(n, dq):
         return pltpu.make_async_remote_copy(
-            src_ref=out3.at[wrap(me_q + dq, NQ)], dst_ref=land3.at[n, me_q], send_sem=s5_send.at[n], recv_sem=s5_recv.at[n],
+            src_ref=out3.at[qs[dq]], dst_ref=land3.at[n, me_q], send_sem=s5_send.at[n], recv_sem=s5_recv.at[n],
             device_id=at(AWAY[n], 0, dq), device_id_type=MESH,
         )
 
@@ -295,26 +308,26 @@
     def take(n):
         all_rows(n).wait_recv()
         share = mm(gather[...], land3[n].reshape(NM * PER, LANES)).astype(BF16)
-        gu[pl.ds(wrap(me_z + ND - AWAY[n], ND) * PER, PER)] = share.reshape(PER, NM, LANES)
+        gu[pl.ds(zs[-AWAY[n] % ND] * PER, PER)] = share.reshape(PER, NM, LANES)
 
     def hop(way, dist, k, received):
         sign = 1 if way == 0 else -1
-        origin = wrap(me_z + ND - sign * (dist if received else parent(dist)), ND)
-        slot = gu.at[origin * PER + k]
+        off = -sign * (dist if received else parent(dist))
+        slot = gu.at[zs[off % ND] * PER + k]
         copy = pltpu.make_async_remote_copy(
             src_ref=slot, dst_ref=slot, send_sem=s3_send.at[way, dist - 1, k], recv_sem=s3_recv.at[way, dist - 1, k],
-            device_id=(wrap(me_z + ND + sign * (dist - parent(dist)), ND), me_m), device_id_type=MESH,
-        )
-        return copy, origin
+            device_id=(zs[sign * (dist - parent(dist)) % ND], me_m), device_id_type=MESH,
+        )
+        return copy, off
 
     def each(dist, received, what, ks=range(PER), ways=(0, 1)):
         for k in ks:
             for way in ways:
                 if dist == HALF and (k < PER // 2) != (way == 0):
                     continue
-                copy, origin = hop(way, dist, k, received)
+                copy, off = hop(way, dist, k, received)
                 if k == PER - 1:
-                    pl.when(has_four(origin))(functools.partial(what, copy))
+                    pl.when(has_four(off))(functools.partial(what, copy))
                 else:
                     what(copy)
 
@@ -353,14 +366,21 @@
 
     back = rb[pl.ds(pl.multiple_of(me_z * CPD, 16), CPD), :]
     zeros = functools.partial(jnp.zeros, dtype=BF16)
-    twice = jnp.concatenate([back, back, zeros((LANES - 2 * CPD, BS))], axis=0)
-    turned_back = mm(lbp[...], mm_nt(scaled[...], twice).astype(BF16))
-    slabs = [turned_back[i * NM : (i + 1) * NM] for i in range(RPD)]
-    lane = lax.broadcasted_iota(jnp.int32, (NM, LANES), 1)
-    pairs = [jnp.where(lane < CPD, slabs[i], slabs[min(i + 1, RPD - 1)]) for i in range(0, RPD, 2)]
-    pairs = jnp.concatenate(pairs, axis=0).astype(BF16)
-    row, col = grid2(NM * 8, 5 * NM)
-    out4[...] = mm(one_hot(col == wrap(row, 8) * NM + row // 8), pairs).reshape(NM, 8, LANES).astype(BF16)
+    wide = jnp.concatenate([back, zeros((LANES - CPD, BS))], axis=0)
+    turned_back = mm(lbp[...], mm_nt(scaled[...], wide).astype(BF16))
+    lane = lax.broadcasted_iota(jnp.int32, (1, LANES), 1)
+    packed = []
+    for q in range(PER):
+        line_q = jnp.zeros((NM, LANES), F32)
+        for i, lo, hi in pieces(q):
+            moved = roll(turned_back[i * NM : (i + 1) * NM], i * CPD - q * LANES)
+            line_q = jnp.where((lane >= lo) & (lane < hi), moved, line_q)
+        packed.append(line_q)
+    packed = jnp.concatenate(packed, axis=0).astype(BF16)
+    row, col = grid2(NM * PER, NM * PER)
+    by_holder = one_hot(col == wrap(row, PER) * NM + row // PER)
+    out4[...] = mm(by_holder, packed).reshape(NM, PER, LANES).astype(BF16)
+
     def spread(src, dst, send_sem, recv_sem):
         for p in PEERS:
             to = peer(p)
@@ -371,10 +391,17 @@
         dst[me_m] = src[me_m]
         return pltpu.make_async_remote_copy(
             src_ref=src.at[pl.ds(0, NM - 1)], dst_ref=dst.at[pl.ds(0, NM - 1)], send_sem=send_sem, recv_sem=recv_sem,
-            device_id=(me_z, wrap(me_m + 1, NM)), device_id_type=MESH,
+            device_id=(me_z, peer((0, 0, 1))), device_id_type=MESH,
         )
 
     done4 = spread(out4, land4, s4_send, s4_recv)
+
+    row, col = grid2(NM * PER, NB)
+    by_owner = one_hot(owner == row // PER)
+    row, col = grid2(PER * NB, NB)
+    at_offset = one_hot(offset == wrap(row, NB))
+    row, col = grid2(PER * NB, NM * PER)
+    place[...] = jnp.where(row // NB == wrap(col, PER), mm_nt(at_offset, by_owner), 0.0).astype(BF16)
 
     row, col = grid2(BS, BS)
     gn[...] = mm(one_hot(row == wrap(col, NM) * RPD + col // NM), block()).astype(BF16)
@@ -390,7 +417,7 @@
     done2.wait_send()
     for n in range(len(AWAY)):
         all_rows(n).wait_send()
-    for dist in range(3, HALF + 1):
+    for dist in (3, 4, 5, 6):
         each(dist, False, wait_send)
     done4.wait_send()
     done4.wait_recv()
@@ -408,11 +435,17 @@
     ]
     for copy in copies[:4]:
         copy.start()
-    returned = land4[...].astype(F32).reshape(NM * 8, LANES).astype(BF16)
-    placed = mm(place[...], returned).astype(BF16)
+    returned = land4[...].astype(F32).reshape(NM * PER, LANES).astype(BF16)
+    placed = mm(place[...], returned)
+    lane = lax.broadcasted_iota(jnp.int32, (1, LANES), 1)
     for i in range(RPD):
-        pair = placed[(i // 2) * NB : (i // 2 + 1) * NB, :]
-        upd[i] = pair[:, (i % 2) * CPD : (i % 2 + 1) * CPD]
+        mine = jnp.zeros((NB, LANES), F32)
+        for q in range(PER):
+            for other, lo, hi in pieces(q):
+                if other == i:
+                    moved = roll(placed[q * NB : (q + 1) * NB], q * LANES - i * CPD)
+                    mine = jnp.where(lane >= q * LANES + lo - i * CPD, moved, mine)
+        upd[i] = mine[:, :CPD].astype(BF16)
     copies[4].start()
     for copy in copies:
         copy.wait()
@@ -427,8 +460,8 @@
     inner = pl.pallas_call(
         kernel,
         out_shape=(
-            pltpu.VMEM((NM, 8, LANES), BF16),
-            pltpu.VMEM((5 * NB, NM * 8), BF16),
+            pltpu.VMEM((NM, PER, LANES), BF16),
+            pltpu.VMEM((PER * NB, NM * PER), BF16),
             pltpu.VMEM((CPD, BS), F32),
             pltpu.VMEM((CPD, BS), F32),
             pltpu.VMEM((BS, BS), BF16),
@@ -454,7 +487,7 @@
             pltpu.VMEM((NQ, NY * PER, LANES), BF16),
             pltpu.VMEM((len(AWAY), NQ, NY * PER, LANES), BF16),
             pltpu.VMEM((ND * PER, NM, LANES), BF16),
-            pltpu.VMEM((NM, 8, LANES), BF16),
+            pltpu.VMEM((NM, PER, LANES), BF16),
             pltpu.VMEM((NM * PER, PER * NB), BF16),
             pltpu.VMEM((NM * PER, NM * PER), BF16),
             pltpu.VMEM((NM * PER, NM * PER), BF16),

time: 64 us -> 63.4 us (level)
  Pallas kernels: 63.2 us -> 62.5 us
    pallas_call x1, Pallas kernels: 61.7 us -> 61 us  [per_device(): pl.pallas_call(kernel, out_shape=(pltpu.VMEM((NM, PER, LANES), BF16), plt...]
where the time goes in v4:
time: 63.4 us; the launch traced here: 63.2 us
  Pallas kernels  62.5 us (99%)
  between operations  0.64 us (1%)
    pallas_call x1, Pallas kernels, per_device(): pl.pallas_call(kernel, out_shape=(pltpu.VMEM((NM, PER, LANES), BF16), plt...  61 us
    pallas_call x1, Pallas kernels, per_device(): pl.pallas_call(finish, out_shape=(jax.ShapeDtypeStruct((RPD, NB, CPD), BF...  1.5 us

profile of v4, /device:TPU:1, one launch (start us, length us, event | category | flops | bytes accessed | tf_op | source)
XLA Modules:
  0.0 63.2 jit_solution(4563429872905650561)
XLA Ops:
  0.6 61.0 %shard_map.128 = (bf16[64,4,128]{2,1,0:T(4,128)(2,1)S(1)}, bf16[128,256]{1,0:T(8,128)(2,1)S(1)}, f32[48,576]{1,0:T(8,128)S(1)}, f32[48,576]{1,0:T(8,128)S(1)}, b...) custom-call(bf16[9,32,576]{2,1,0:T(8,128)(2,1)} %bitcast.28, s32[1,32]{1,0:T(1,128)} %bitcast.31, s32[1,32]{1,0:T(1,128)} %bitcast.32, ...), custom_call_target="tpu_custom_call" | custom-call | tf_op jit(solution)/shard_map/pallas_call | solution.py:460
  61.7 1.5 %shard_map.129 = (bf16[9,32,48]{2,1,0:T(8,128)(2,1)}, f32[48,576]{1,0:T(8,128)}, f32[48,576]{1,0:T(8,128)}, bf16[576,576]{1,0:T(8,128)(2,1)}, f32[576,576]{1,0:T(8,128)}) custom-call(bf16[64,4,128]{2,1,0:T(4,128)(2,1)S(1)} %get-tuple-element.16.land4, bf16[128,256]{1,0:T(8,128)(2,1)S(1)} %get-tuple-element.17.place, f32[48,576]{1,0:T(8,128)S(1)} %get-tuple-element.18.nlf, ...), custom_call_target="tpu_custom_call" | custom-call | tf_op jit(solution)/shard_map/pallas_call | solution.py:526
